TPU v7x, 32 devices: a whole 2x2x4 slice. The times are simulated.
32 devices in a mesh: dp: 4 (over z), rows: 8 (over y, x, core).
Axes of the slice: x: 2, y: 2, z: 4, core: 2. Of those that a mesh axis runs over, the one named last changes fastest.
Arguments:
- latent: bfloat16 [8, 8, 64, 640], P('dp', 'rows'), may hold values from -16.25 to 16.25
- hidden: bfloat16 [8, 8, 64, 640], P('dp', 'rows'), may hold values from -16.25 to 16.25
- cotangent: bfloat16 [8, 8, 64, 640], P('dp', 'rows'), may hold values from -6 to 6
- filter_one: bfloat16 [9, 640, 640], P(None, 'dp', 'rows'), may hold values from -0.078125 to 0.078125
- filter_two: bfloat16 [9, 640, 640], P(None, 'dp', 'rows'), may hold values from -0.078125 to 0.078125
- gain_one: float32 [640], replicated, may hold values from 0.1 to 1.9
- shift_one: float32 [640], replicated, may hold values from -2.5 to 2.5
- gain_two: float32 [640], replicated, may hold values from 0.1 to 1.9
- shift_two: float32 [640], replicated, may hold values from -2.5 to 2.5
Outputs:
- latent_grad: bfloat16 [8, 8, 64, 640], P('dp', 'rows')
All inputs are finite; a program needn't handle non-finite values.
Results may differ from a plain program's by a relative error of at most 0.0027.
Values may be sent and summed in bfloat16 or wider, within the bound.
A program may use at most 128 MiB of HBM per device.

v0:
```python
import functools

import jax
import jax.numpy as jnp
from jax import lax
from jax.experimental import pallas as pl
from jax.experimental.pallas import tpu as pltpu
from jax.sharding import PartitionSpec as P

GROUPS = 16
GSIZE = 40
TAPS = 9
MESH = pl.DeviceIdType.MESH


def extended(block, sides, width):
    for axis, dim in sides:
        count = lax.axis_size(axis)
        forward = [(i, i + 1) for i in range(count - 1)]
        backward = [(target, source) for source, target in forward]
        low = lax.ppermute(
            lax.slice_in_dim(block, block.shape[dim] - width, None, axis=dim), axis, forward
        )
        high = lax.ppermute(lax.slice_in_dim(block, 0, width, axis=dim), axis, backward)
        block = jnp.concatenate([low, block, high], axis=dim)
    return block


def group_sums(values):
    per_channel = jnp.sum(values, axis=(1, 2))
    return jnp.sum(per_channel.reshape(per_channel.shape[0], GROUPS, -1), axis=2)


def expand_groups(moment):
    return jnp.repeat(moment, GSIZE, axis=1)[:, None, None, :]


def finish_stats(sum_plain, sum_square, number):
    average = sum_plain / number
    variance = sum_square / number - average * average
    return (average, lax.rsqrt(variance + 1e-05))


def reduced_stats(field, number):
    values = field.astype(jnp.float32)
    sum_plain, sum_square = lax.psum((group_sums(values), group_sums(values * values)), "rows")
    return finish_stats(sum_plain, sum_square, number)


def norm_backward(field, stats, gain, shift, incoming, number):
    average, inverse = stats
    values = field.astype(jnp.float32)
    normed = (values - expand_groups(average)) * expand_groups(inverse)
    linear = normed * gain + shift
    logistic = jax.nn.sigmoid(linear)
    scaled = incoming * logistic * (1.0 + linear * (1.0 - logistic)) * gain
    sum_first, sum_second = lax.psum((group_sums(scaled), group_sums(scaled * normed)), "rows")
    first = sum_first / number
    second = sum_second / number
    return expand_groups(inverse) * (scaled - expand_groups(first) - normed * expand_groups(second))


def conv_backward(gradient, weights):
    images, rows_here, breadth, channels = gradient.shape
    padded = extended(gradient, (("rows", 1),), 1)
    padded = jnp.pad(padded, ((0, 0), (0, 0), (1, 1), (0, 0)))
    pixels = images * rows_here * breadth
    shifted = []
    for tap_index in range(9):
        down_step = tap_index // 3 - 1
        side_step = tap_index % 3 - 1
        window = padded[
            :, 1 - down_step : 1 - down_step + rows_here, 1 - side_step : 1 - side_step + breadth, :
        ]
        shifted.append(window.reshape(pixels, channels))
    stacked = jnp.stack(shifted, axis=1)
    gathered = lax.all_gather(weights, "dp", axis=1, tiled=True)
    section = lax.all_gather(gathered, "rows", axis=2, tiled=True)
    columns = section.shape[2]
    window = stacked.reshape(pixels, 9 * columns)
    flat = jnp.transpose(section, (0, 2, 1)).reshape(9 * columns, section.shape[1])
    result = jnp.dot(window, flat, preferred_element_type=jnp.float32)
    return result.reshape(images, rows_here, breadth, channels)


def plain_body(
    latent, hidden, cotangent, filter_one, filter_two, gain_one, shift_one, gain_two, shift_two
):
    number = latent.shape[1] * lax.axis_size("rows") * latent.shape[2] * GSIZE
    stats_two = reduced_stats(hidden, number)
    back_two = conv_backward(cotangent, filter_two)
    hidden_grad = norm_backward(hidden, stats_two, gain_two, shift_two, back_two, number).astype(
        jnp.bfloat16
    )
    stats_one = reduced_stats(latent, number)
    back_one = conv_backward(hidden_grad, filter_one)
    latent_part = norm_backward(latent, stats_one, gain_one, shift_one, back_one, number)
    return (cotangent.astype(jnp.float32) + latent_part).astype(jnp.bfloat16)


def kernel(
    depth, rows, breadth,
    lat_ref, hid_ref, cot_ref, raw1, raw2, gain1, shift1, gain2, shift2,
    out_ref,
    x_cot, x_hg, lat_t, hid_t, lat_b, hid_b, stage1, stage2, w1, w2, wt, y_ref, back, out_b, out_t,
    f1_ref, f2_ref, par_ref,
    z_send, z_recv, w_send, w_recv, c_send, c_recv, g_send, g_recv,
    a_send, a_recv, o_send, o_recv,
):
    d = lax.axis_index("dp")
    r = lax.axis_index("rows")
    channels, lanes = x_cot.shape[1:]
    block = channels // rows
    images = lanes // breadth
    halves = rows // depth
    wide = w1.shape[2]
    number = rows * breadth * GSIZE

    def place(index):
        return index + lax.rem(index, 2) * (rows - 2 * index)

    def rows_of(index):
        return pl.ds(pl.multiple_of(place(index) * block, block), block)

    def arrange(raw, ready):
        for k in range(halves):
            ready[k, :, TAPS * block :] = jnp.zeros((block, wide - TAPS * block), jnp.bfloat16)
        for tap in range(TAPS):
            turned = raw[tap].T
            for k in range(halves):
                ready[k, :, tap * block : (tap + 1) * block] = turned[:, k * block : (k + 1) * block]

    def remote(src, dst, send, recv, **device):
        return pltpu.make_async_remote_copy(
            src_ref=src, dst_ref=dst, send_sem=send, recv_sem=recv,
            device_id=device, device_id_type=MESH,
        )

    barrier = pltpu.get_barrier_semaphore()
    for off in range(1, depth):
        pl.semaphore_signal(barrier, inc=1, device_id={"dp": lax.rem(d + off, depth)}, device_id_type=MESH)
    for off in range(1, rows):
        pl.semaphore_signal(barrier, inc=1, device_id={"rows": lax.rem(r + off, rows)}, device_id_type=MESH)

    arrange(raw2, f2_ref)
    x_cot[r] = cot_ref[...].T
    hid_t[...] = hid_ref[...].T
    lat_t[...] = lat_ref[...].T
    pl.semaphore_wait(barrier, depth - 1 + rows - 1)

    pending = []

    def z_hop(which, src, stage, origin, k, way):
        to = d + 1 - 2 * way
        return remote(
            src, stage.at[origin, k], z_send.at[which, way, origin, k], z_recv.at[which, origin, k], dp=to
        )

    def start_z(which, src, stage):
        for k in range(halves):
            @pl.when(d < depth - 1)
            def _():
                z_hop(which, src.at[k], stage, d, k, 0).start()

            @pl.when(d > 0)
            def _():
                z_hop(which, src.at[k], stage, d, k, 1).start()

    def wait_z_sends(which, src, stage):
        for origin in range(depth):
            for k in range(halves):
                @pl.when((d < depth - 1) & (origin <= d))
                def _():
                    z_hop(which, src.at[k], stage, origin, k, 0).wait_send()

                @pl.when((d > 0) & (origin >= d))
                def _():
                    z_hop(which, src.at[k], stage, origin, k, 1).wait_send()

    def start_exchange(which, src, dst):
        for off in range(1, rows):
            to = lax.rem(r + off, rows)
            copy = remote(
                src.at[rows_of(to), :], dst.at[r],
                a_send.at[which, to], a_recv.at[which, r], rows=to,
            )
            copy.start()
            pending.append(copy)
        dst[r] = src[rows_of(r), :]

    def wait_exchange(which, src, dst):
        for off in range(1, rows):
            frm = lax.rem(r + off, rows)
            remote(src.at[pl.ds(0, block), :], dst.at[frm], a_send.at[which, frm], a_recv.at[which, frm], rows=frm).wait_recv()

    def send_piece(which, origin, k, piece, w):
        to = place(origin * halves + k)

        @pl.when(to != r)
        def _():
            remote(piece, w.at[r], w_send.at[which, to], w_recv.at[which, r], rows=to).start()

        @pl.when(to == r)
        def _():
            w[r] = piece[...]

    def send_own(which, src, w):
        for k in range(halves):
            send_piece(which, d, k, src.at[k], w)

    def wait_piece_sends(which, src, w):
        for off in range(1, rows):
            to = lax.rem(r + off, rows)
            remote(src.at[0], w.at[r], w_send.at[which, to], w_recv.at[which, r], rows=to).wait_send()

    def relay_filters(which, stage, w, off):
        for k in range(halves):
            for way in range(2):
                origin = d - off if way == 0 else d + off

                @pl.when((origin >= 0) & (origin < depth))
                def _():
                    hop = z_hop(which, stage.at[origin, k], stage, origin, k, way)
                    hop.wait_recv()

                    @pl.when((d < depth - 1) if way == 0 else (d > 0))
                    def _():
                        hop.start()

                    send_piece(which, origin, k, stage.at[origin, k], w)

    def wait_filters(which, src, w):
        for off in range(1, rows):
            frm = lax.rem(r + off, rows)
            remote(src.at[0], w.at[frm], w_send.at[which, frm], w_recv.at[which, frm], rows=frm).wait_recv()

    parity = lax.rem(r, 2)
    sibling = r + 1 - 2 * parity

    def gather_send(at, send, recv):
        for off in range(1, rows // 2):
            to = lax.rem(r + 2 * off, rows)
            copy = remote(at(r), at(r), send.at[to], recv.at[r], rows=to)
            copy.start()
            pending.append(copy)
        copy = remote(at(r), at(r), send.at[sibling], recv.at[r], rows=sibling)
        copy.start()
        pending.append(copy)

    def gather_relay(at, send, recv):
        for off in range(1, rows // 2):
            frm = lax.rem(r + 2 * off, rows)
            remote(at(frm), at(frm), send.at[frm], recv.at[frm], rows=frm).wait_recv()
            twin = lax.rem(sibling + 2 * off, rows)
            copy = remote(at(frm), at(frm), send.at[twin], recv.at[frm], rows=sibling)
            copy.start()
            pending.append(copy)

    def gather_wait(at, send, recv):
        for off in range(0, rows // 2):
            frm = lax.rem(sibling + 2 * off, rows)
            remote(at(frm), at(frm), send.at[frm], recv.at[frm], rows=sibling).wait_recv()

    def cot_at(h):
        return x_cot.at[h]

    def hg_at(owner):
        return x_hg.at[:, rows_of(owner), :]

    start_z(0, f2_ref, stage2)
    gather_send(cot_at, c_send, c_recv)
    start_exchange(0, hid_t, hid_b)
    send_own(0, f2_ref, w2)
    arrange(raw1, f1_ref)
    raw_params = [p[...].reshape(1, channels) for p in (gain1, shift1, gain2, shift2)]
    par_ref[...] = jnp.concatenate(raw_params + raw_params, axis=0).T

    lane = lax.broadcasted_iota(jnp.int32, (1, lanes), 1)
    column = lax.rem(lane, breadth)
    image_of = lax.div(lane, breadth)
    groups = block // GSIZE

    def group_means(sums):
        per_lane = jnp.sum(sums.reshape(groups, GSIZE, lanes), axis=1)
        total = jnp.zeros_like(per_lane)
        for image in range(images):
            mine = image_of == image
            part = jnp.sum(jnp.where(mine, per_lane, 0.0), axis=1, keepdims=True)
            total = jnp.where(mine, part, total)
        total = total * (1.0 / number)
        return jnp.broadcast_to(total[:, None, :], (groups, GSIZE, lanes)).reshape(block, lanes)

    def stats(field):
        plain = jnp.zeros((block, lanes), jnp.float32)
        square = jnp.zeros((block, lanes), jnp.float32)
        for h in range(rows):
            values = field[h].astype(jnp.float32)
            plain += values
            square += values * values
        average = group_means(plain)
        variance = group_means(square) - average * average
        return average, lax.rsqrt(variance + 1e-05)

    params = par_ref[rows_of(r), :]

    def conv(x, w):
        wt[...] = w[...].reshape(channels, wide).T
        for h in range(0, rows, 2):
            pair = jnp.concatenate([x[h], x[h + 1]], axis=1)
            result = jnp.dot(wt[...], pair, preferred_element_type=jnp.float32)
            y_ref[h] = result[:, :lanes]
            y_ref[h + 1] = result[:, lanes:]

    def back_at(h):
        sums = []
        for side in range(3):
            total = None
            for down in range(3):
                source = h - (down - 1)
                if 0 <= source < rows:
                    tap = 3 * down + side
                    term = y_ref[source, tap * block : (tap + 1) * block, :]
                    total = term if total is None else total + term
            sums.append(total)
        left = jnp.where(column == breadth - 1, 0.0, pltpu.roll(sums[0], lanes - 1, 1))
        right = jnp.where(column == 0, 0.0, pltpu.roll(sums[2], 1, 1))
        return sums[1] + left + right

    def norm(field, moments, gain, shift, finish):
        average, inverse = moments
        sum_first = jnp.zeros((block, lanes), jnp.float32)
        sum_second = jnp.zeros((block, lanes), jnp.float32)
        for h in range(rows):
            normed = (field[h].astype(jnp.float32) - average) * inverse
            linear = normed * gain + shift
            logistic = 1.0 / (1.0 + jnp.exp(-linear))
            scaled = back_at(h) * logistic * (1.0 + linear * (1.0 - logistic)) * gain
            back[h] = scaled
            sum_first += scaled
            sum_second += scaled * normed
        first = group_means(sum_first)
        second = group_means(sum_second)
        for h in range(rows):
            normed = (field[h].astype(jnp.float32) - average) * inverse
            finish(h, inverse * (back[h] - first - normed * second))

    relay_filters(0, stage2, w2, 1)
    gather_relay(cot_at, c_send, c_recv)
    start_exchange(1, lat_t, lat_b)
    relay_filters(0, stage2, w2, 2)
    wait_exchange(0, hid_t, hid_b)
    moments_two = stats(hid_b)
    start_z(1, f1_ref, stage1)
    for off in range(3, depth):
        relay_filters(0, stage2, w2, off)
    gather_wait(cot_at, c_send, c_recv)
    wait_filters(0, f2_ref, w2)

    conv(x_cot, w2)
    send_own(1, f1_ref, w1)
    relay_filters(1, stage1, w1, 1)
    mine = rows_of(r)

    def finish_two(h, value):
        x_hg[h, mine, :] = value.astype(jnp.bfloat16)

    norm(hid_b, moments_two, params[:, 2:3], params[:, 3:4], finish_two)
    gather_send(hg_at, g_send, g_recv)
    wait_exchange(1, lat_t, lat_b)
    moments_one = stats(lat_b)
    relay_filters(1, stage1, w1, 2)
    for off in range(3, depth):
        relay_filters(1, stage1, w1, off)
    gather_relay(hg_at, g_send, g_recv)
    gather_wait(hg_at, g_send, g_recv)
    wait_filters(1, f1_ref, w1)

    conv(x_hg, w1)

    def finish_one(h, value):
        out_b[h] = (x_cot[h, mine, :].astype(jnp.float32) + value).astype(jnp.bfloat16)

    norm(lat_b, moments_one, params[:, 0:1], params[:, 1:2], finish_one)
    for off in range(1, rows):
        to = lax.rem(r + off, rows)
        copy = remote(out_b.at[to], out_t.at[place(r)], o_send.at[to], o_recv.at[r], rows=to)
        copy.start()
        pending.append(copy)
    out_t[place(r)] = out_b[r]
    for off in range(1, rows):
        frm = lax.rem(r + off, rows)
        remote(out_b.at[frm], out_t.at[place(frm)], o_send.at[frm], o_recv.at[frm], rows=frm).wait_recv()
    out_ref[...] = out_t[...].reshape(channels, lanes).T
    for copy in pending:
        copy.wait_send()
    wait_z_sends(0, f2_ref, stage2)
    wait_z_sends(1, f1_ref, stage1)
    wait_piece_sends(0, f2_ref, w2)
    wait_piece_sends(1, f1_ref, w1)


def kernel_body(
    depth, rows,
    latent, hidden, cotangent, filter_one, filter_two, gain_one, shift_one, gain_two, shift_two,
):
    images, _, breadth, channels = latent.shape
    lanes = images * breadth
    block = channels // rows
    halves = rows // depth
    wide = -(-TAPS * block // 128) * 128
    bf16, f32 = jnp.bfloat16, jnp.float32
    dma = pltpu.SemaphoreType.DMA
    out = pl.pallas_call(
        functools.partial(kernel, depth, rows, breadth),
        out_shape=jax.ShapeDtypeStruct((lanes, channels), bf16),
        in_specs=[pl.BlockSpec(memory_space=pltpu.VMEM)] * 9,
        out_specs=pl.BlockSpec(memory_space=pltpu.VMEM),
        scratch_shapes=[
            pltpu.VMEM((rows, channels, lanes), bf16),
            pltpu.VMEM((rows, channels, lanes), bf16),
            pltpu.VMEM((channels, lanes), bf16),
            pltpu.VMEM((channels, lanes), bf16),
            pltpu.VMEM((rows, block, lanes), bf16),
            pltpu.VMEM((rows, block, lanes), bf16),
            pltpu.VMEM((depth, halves, block, wide), bf16),
            pltpu.VMEM((depth, halves, block, wide), bf16),
            pltpu.VMEM((rows, block, wide), bf16),
            pltpu.VMEM((rows, block, wide), bf16),
            pltpu.VMEM((wide, channels), bf16),
            pltpu.VMEM((rows, wide, lanes), f32),
            pltpu.VMEM((rows, block, lanes), f32),
            pltpu.VMEM((rows, block, lanes), bf16),
            pltpu.VMEM((rows, block, lanes), bf16),
            pltpu.VMEM((halves, block, wide), bf16),
            pltpu.VMEM((halves, block, wide), bf16),
            pltpu.VMEM((channels, 8), f32),
            dma((2, 2, depth, halves)), dma((2, depth, halves)),
            dma((2, rows)), dma((2, rows)),
            dma((rows,)), dma((rows,)),
            dma((rows,)), dma((rows,)),
            dma((2, rows)), dma((2, rows)),
            dma((rows,)), dma((rows,)),
        ],
        compiler_params=pltpu.CompilerParams(collective_id=0, has_side_effects=True),
    )(
        latent.reshape(lanes, channels), hidden.reshape(lanes, channels),
        cotangent.reshape(lanes, channels), filter_one, filter_two,
        gain_one, shift_one, gain_two, shift_two,
    )
    return out.reshape(latent.shape)


def solution(mesh):
    depth, rows = mesh.shape["dp"], mesh.shape["rows"]
    in_specs = (
        P("dp", "rows", None, None),
        P("dp", "rows", None, None),
        P("dp", "rows", None, None),
        P(None, "dp", "rows"),
        P(None, "dp", "rows"),
        P(),
        P(),
        P(),
        P(),
    )

    def body(latent, *rest):
        images, rows_here, breadth, channels = latent.shape
        fits = (
            rows_here == 1
            and images * breadth == 128
            and depth > 2
            and rows == 2 * depth
            and rows % 2 == 0
            and channels % (rows * GSIZE) == 0
            and (channels // rows) % 16 == 0
            and channels % 128 == 0
        )
        if fits:
            return kernel_body(depth, rows, latent, *rest)
        return plain_body(latent, *rest)

    return jax.shard_map(
        body, mesh=mesh, in_specs=in_specs, out_specs=P("dp", "rows", None, None), check_vma=False
    )
```

profile of v0, /device:TPU:0, one launch (start us, length us, event | category | flops | bytes accessed | tf_op | source)
XLA Modules:
  0.0 58.5 jit_solution(16518307797098665622)
XLA Ops:
  0.0 56.9 %shard_map.91 = bf16[128,640]{1,0:T(8,128)(2,1)} custom-call(bf16[128,640]{1,0:T(8,128)(2,1)} %bitcast.7, bf16[128,640]{1,0:T(8,128)(2,1)} %bitcast.8, bf16[128,640]{1,0:T(8,128)(2,1)} %bitcast.9, bf16[9,160,80]{2,1,0:T(8,128)(2,1)} %raw1.1, bf16[9,160,80]{2,1,0:T(8,128)(2,1)} %raw2.1, f32[640]{0:T(1024)} %gain1.1, f32[640]{0:T(1024)} %shift1.1, f32[640]{0:T(1024)} %gain2.1, ...), custom_call_target="tpu_custom_call" | custom-call | tf_op jit(solution)/shard_map/pallas_call | solution.py:413
  56.9 1.6 %copy.12 = bf16[2,1,64,640]{3,2,1,0:T(8,128)(2,1)} copy(bf16[2,1,64,640]{3,2,1,0:T(8,128)(2,1)} %bitcast.6) | data formatting | bytes 327680
where the time goes:
time: 58.7 us; the launch traced here: 58.5 us
  Pallas kernels  56.9 us (97%)
  local copies, waits for them, and re-layouts  1.6 us (3%)
    pallas_call x1, Pallas kernels, kernel_body(): pl.pallas_call(functools.partial(kernel, depth, rows, breadth), out_shape...  56.9 us
    unnamed x1, local copies, waits for them, and re-layouts  1.6 us

commit v1 on v0

v1 whole, which is shorter than its diff:
```python
import functools

import jax
import jax.numpy as jnp
from jax import lax
from jax.experimental import pallas as pl
from jax.experimental.pallas import tpu as pltpu
from jax.sharding import PartitionSpec as P

GROUPS = 16
GSIZE = 40
TAPS = 9
MESH = pl.DeviceIdType.MESH


def extended(block, sides, width):
    for axis, dim in sides:
        count = lax.axis_size(axis)
        forward = [(i, i + 1) for i in range(count - 1)]
        backward = [(target, source) for source, target in forward]
        low = lax.ppermute(
            lax.slice_in_dim(block, block.shape[dim] - width, None, axis=dim), axis, forward
        )
        high = lax.ppermute(lax.slice_in_dim(block, 0, width, axis=dim), axis, backward)
        block = jnp.concatenate([low, block, high], axis=dim)
    return block


def group_sums(values):
    per_channel = jnp.sum(values, axis=(1, 2))
    return jnp.sum(per_channel.reshape(per_channel.shape[0], GROUPS, -1), axis=2)


def expand_groups(moment):
    return jnp.repeat(moment, GSIZE, axis=1)[:, None, None, :]


def finish_stats(sum_plain, sum_square, number):
    average = sum_plain / number
    variance = sum_square / number - average * average
    return (average, lax.rsqrt(variance + 1e-05))


def reduced_stats(field, number):
    values = field.astype(jnp.float32)
    sum_plain, sum_square = lax.psum((group_sums(values), group_sums(values * values)), "rows")
    return finish_stats(sum_plain, sum_square, number)


def norm_backward(field, stats, gain, shift, incoming, number):
    average, inverse = stats
    values = field.astype(jnp.float32)
    normed = (values - expand_groups(average)) * expand_groups(inverse)
    linear = normed * gain + shift
    logistic = jax.nn.sigmoid(linear)
    scaled = incoming * logistic * (1.0 + linear * (1.0 - logistic)) * gain
    sum_first, sum_second = lax.psum((group_sums(scaled), group_sums(scaled * normed)), "rows")
    first = sum_first / number
    second = sum_second / number
    return expand_groups(inverse) * (scaled - expand_groups(first) - normed * expand_groups(second))


def conv_backward(gradient, weights):
    images, rows_here, breadth, channels = gradient.shape
    padded = extended(gradient, (("rows", 1),), 1)
    padded = jnp.pad(padded, ((0, 0), (0, 0), (1, 1), (0, 0)))
    pixels = images * rows_here * breadth
    shifted = []
    for tap_index in range(9):
        down_step = tap_index // 3 - 1
        side_step = tap_index % 3 - 1
        window = padded[
            :, 1 - down_step : 1 - down_step + rows_here, 1 - side_step : 1 - side_step + breadth, :
        ]
        shifted.append(window.reshape(pixels, channels))
    stacked = jnp.stack(shifted, axis=1)
    gathered = lax.all_gather(weights, "dp", axis=1, tiled=True)
    section = lax.all_gather(gathered, "rows", axis=2, tiled=True)
    columns = section.shape[2]
    window = stacked.reshape(pixels, 9 * columns)
    flat = jnp.transpose(section, (0, 2, 1)).reshape(9 * columns, section.shape[1])
    result = jnp.dot(window, flat, preferred_element_type=jnp.float32)
    return result.reshape(images, rows_here, breadth, channels)


def plain_body(
    latent, hidden, cotangent, filter_one, filter_two, gain_one, shift_one, gain_two, shift_two
):
    number = latent.shape[1] * lax.axis_size("rows") * latent.shape[2] * GSIZE
    stats_two = reduced_stats(hidden, number)
    back_two = conv_backward(cotangent, filter_two)
    hidden_grad = norm_backward(hidden, stats_two, gain_two, shift_two, back_two, number).astype(
        jnp.bfloat16
    )
    stats_one = reduced_stats(latent, number)
    back_one = conv_backward(hidden_grad, filter_one)
    latent_part = norm_backward(latent, stats_one, gain_one, shift_one, back_one, number)
    return (cotangent.astype(jnp.float32) + latent_part).astype(jnp.bfloat16)


def kernel(
    depth, rows, breadth,
    lat_ref, hid_ref, cot_ref, raw1, raw2, gain1, shift1, gain2, shift2,
    out_ref,
    cot_t, x_cot, hid_s, hid_b, w1, w2, s1, s2, r1,
    xs1, xs2, y_ref, p1, q1, p2, q2, hg_s, hg_r,
    nrm1, act1, nrm2, act2, inv2_ref, st_s, st_b, par_ref,
    z_send, z_recv, f_send, f_recv, b_send, b_recv, c_send, c_recv, h_send, h_recv,
    p_send, p_recv, g_send, g_recv, o_send, o_recv, t_send, t_recv,
):
    d = lax.axis_index("dp")
    r = lax.axis_index("rows")
    chips = rows // 2
    c = r // 2
    k = lax.rem(r, 2)
    sibling = r + 1 - 2 * k
    channels, lanes = cot_t.shape
    block = channels // depth
    half = block // 2
    images = lanes // breadth
    wide = w1.shape[3]
    number = rows * breadth * GSIZE
    groups = channels // GSIZE
    bf16, f32 = jnp.bfloat16, jnp.float32

    def remote(src, dst, send, recv, **device):
        return pltpu.make_async_remote_copy(
            src_ref=src, dst_ref=dst, send_sem=send, recv_sem=recv,
            device_id=device, device_id_type=MESH,
        )

    barrier = pltpu.get_barrier_semaphore()

    @pl.when(d > 0)
    def _():
        pl.semaphore_signal(barrier, inc=1, device_id={"dp": d - 1}, device_id_type=MESH)

    @pl.when(d < depth - 1)
    def _():
        pl.semaphore_signal(barrier, inc=1, device_id={"dp": d + 1}, device_id_type=MESH)

    for off in range(1, rows):
        pl.semaphore_signal(barrier, inc=1, device_id={"rows": lax.rem(r + off, rows)}, device_id_type=MESH)

    pending = []

    def arrange(ready, raw, which):
        start = pl.multiple_of(which * half, 16)
        pad = wide - 3 * half
        ready[:, 3 * half :] = jnp.zeros((3 * half, pad), bf16)
        for tap in range(TAPS):
            down, side = tap // 3, tap % 3
            ready[down * half : (down + 1) * half, side * half : (side + 1) * half] = raw[
                tap, pl.ds(start, half), :
            ]

    arrange(w2.at[d, k], raw2, k)
    arrange(s2, raw2, 1 - k)

    beside = jnp.where((d > 0) & (d < depth - 1), 2, 1)
    pl.semaphore_wait(barrier, rows - 1 + beside)

    def hop(which, w, origin, part, way):
        return remote(
            w.at[origin, part], w.at[origin, part],
            z_send.at[which, way, origin, part], z_recv.at[which, origin, part], dp=d + 1 - 2 * way,
        )

    def can(way):
        return (d < depth - 1) if way == 0 else (d > 0)

    def start_hops(which, w, part, ways=(0, 1)):
        for way in ways:
            @pl.when(can(way))
            def _():
                hop(which, w, d, part, way).start()

    start_hops(0, w2, k)
    twin = remote(s2, w2.at[d, k], b_send.at[0], b_recv.at[0], rows=sibling)
    twin.start()
    pending.append(twin)

    cot_t[...] = cot_ref[...].T

    def piece_of(to):
        return cot_t.at[pl.ds(pl.multiple_of((to // 2) * block, block), block), :]

    for off in range(1, rows):
        to = lax.rem(r + off, rows)
        copy = remote(piece_of(to), x_cot.at[r], c_send.at[to], c_recv.at[r], rows=to)
        copy.start()
        pending.append(copy)
    x_cot[r] = piece_of(r)[...]

    remote(s2, w2.at[d, 1 - k], b_send.at[0], b_recv.at[0], rows=sibling).wait_recv()
    start_hops(0, w2, 1 - k)

    hid_full = hid_ref[...].astype(f32).T
    for to in range(rows):
        parts = [
            hid_full[block * b + GSIZE * (to // 2) : block * b + GSIZE * (to // 2 + 1)]
            for b in (to % 2, to % 2 + 2)
        ]
        hid_s[to] = jnp.concatenate(parts, axis=0).astype(bf16)
    for off in range(1, rows):
        to = lax.rem(r + off, rows)
        copy = remote(hid_s.at[to], hid_b.at[r], h_send.at[to], h_recv.at[r], rows=to)
        copy.start()
        pending.append(copy)
    hid_b[r] = hid_s[r]

    for part in range(2):
        for side_core in range(2):
            ready = s1.at[part, side_core]
            ready[:, 3 * GSIZE :] = jnp.zeros((3 * half, ready.shape[1] - 3 * GSIZE), bf16)
            for tap in range(TAPS):
                down, side = tap // 3, tap % 3
                ready[down * half : (down + 1) * half, side * GSIZE : (side + 1) * GSIZE] = raw1[
                    tap, side_core * half : (side_core + 1) * half, part * GSIZE : (part + 1) * GSIZE
                ]

    def each_shuffle(act):
        for part in range(2):
            for side_core in range(2):
                to = 2 * (2 * k + part) + side_core
                src = s1.at[part, side_core]

                @pl.when(to != r)
                def _():
                    act(remote(src, r1.at[c], f_send.at[part, side_core], f_recv.at[c], rows=to))

                yield to, src

    for to, src in each_shuffle(lambda copy: copy.start()):
        @pl.when(to == r)
        def _():
            r1[c] = src[...]

    lane = lax.broadcasted_iota(jnp.int32, (1, lanes), 1)
    column = lax.rem(lane, breadth)
    image_of = lax.div(lane, breadth)
    first_half = lax.rem(lane, breadth) < breadth // 2

    def image_totals(per_lane):
        total = jnp.zeros_like(per_lane)
        for image in range(images):
            mine = image_of == image
            part = jnp.sum(jnp.where(mine, per_lane, 0.0), axis=1, keepdims=True)
            total = jnp.where(mine, part, total)
        return total

    def pack_sums(one, two):
        return jnp.where(first_half, image_totals(one), image_totals(two))

    def send_sums(which, packed):
        st_s[which] = packed
        for off in range(1, rows):
            to = lax.rem(r + off, rows)
            copy = remote(st_s.at[which], st_b.at[which, r], t_send.at[which, to], t_recv.at[which, r], rows=to)
            copy.start()
            pending.append(copy)
        st_b[which, r] = packed

    def wait_sums(which):
        for off in range(1, rows):
            frm = lax.rem(r + off, rows)
            remote(
                st_s.at[which], st_b.at[which, frm], t_send.at[which, frm], t_recv.at[which, frm], rows=frm
            ).wait_recv()
        total = st_b[which, 0]
        for h in range(1, rows):
            total = total + st_b[which, h]
        total = total * (1.0 / number)
        quarter = breadth // 2
        ahead = pltpu.roll(total, lanes - quarter, 1)
        behind = pltpu.roll(total, quarter, 1)
        one = jnp.where(first_half, total, behind)
        two = jnp.where(first_half, ahead, total)
        return one, two

    def spread(moment):
        return jnp.broadcast_to(moment[:, None, :], (groups, GSIZE, lanes)).reshape(channels, lanes)

    def by_group(values):
        return jnp.sum(values.reshape(groups, GSIZE, lanes), axis=1)

    nrm1[...] = lat_ref[...].astype(f32).T
    send_sums(0, pack_sums(by_group(nrm1[...]), by_group(nrm1[...] * nrm1[...])))

    raw_params = [p[...].reshape(1, channels) for p in (gain1, shift1, gain2, shift2)]
    par_ref[...] = jnp.concatenate(raw_params + raw_params, axis=0).T

    def store_shifts(xs, part, h, values):
        left = jnp.where(column == breadth - 1, 0.0, pltpu.roll(values, lanes - 1, 1))
        right = jnp.where(column == 0, 0.0, pltpu.roll(values, 1, 1))
        xs[part, h, 0:half] = left.astype(bf16)
        xs[part, h, half : 2 * half] = values.astype(bf16)
        xs[part, h, 2 * half : 3 * half] = right.astype(bf16)

    for xs in (xs1, xs2):
        for part in range(2):
            for h in range(rows):
                xs[part, h, 3 * half :] = jnp.zeros((wide - 3 * half, lanes), bf16)

    def wait_exchange(src, dst, send, recv):
        for off in range(1, rows):
            frm = lax.rem(r + off, rows)
            remote(src, dst.at[frm], send.at[frm], recv.at[frm], rows=frm).wait_recv()

    wait_exchange(piece_of(r), x_cot, c_send, c_recv)
    for h in range(rows):
        values = x_cot[h].astype(f32)
        for part in range(2):
            store_shifts(xs2, part, h, values[part * half : (part + 1) * half])

    def conv(w, origin, xs):
        for h in range(0, rows, 2):
            total = None
            for part in range(2):
                pair = jnp.concatenate([xs[part, h], xs[part, h + 1]], axis=1)
                term = jnp.dot(w[origin, part], pair, preferred_element_type=f32)
                total = term if total is None else total + term
            y_ref[h] = total[:, :lanes]
            y_ref[h + 1] = total[:, lanes:]

    def row_of(h):
        total = y_ref[h, half : 2 * half]
        if h + 1 < rows:
            total = total + y_ref[h + 1, 0:half]
        if h > 0:
            total = total + y_ref[h - 1, 2 * half : 3 * half]
        return total

    def each_part(origin, act):
        for j in range(2):
            to = 2 * (2 * k + j) + lax.rem(origin, 2)
            slot = origin // 2

            @pl.when(to != r)
            def _():
                act(remote(
                    p1.at[origin, j], q1.at[slot, c], p_send.at[origin, j], p_recv.at[slot, c], rows=to
                ))

            yield j, to, slot

    def conv_two(origin):
        conv(w2, origin, xs2)
        for h in range(0, rows, 2):
            low, high = row_of(h), row_of(h + 1)
            for j in range(2):
                both = [low[j * GSIZE : (j + 1) * GSIZE], high[j * GSIZE : (j + 1) * GSIZE]]
                p1[origin, j, h // 2] = jnp.concatenate(both, axis=0).astype(bf16)
        for j, to, slot in each_part(origin, lambda copy: copy.start()):
            @pl.when(to == r)
            def _():
                q1[slot, c] = p1[origin, j]

    def conv_one(origin):
        conv(w1, origin, xs1)
        for h in range(rows):
            p2[origin, h] = row_of(h).astype(bf16)
        for off in range(1, rows):
            to = lax.rem(r + off, rows)
            remote(p2.at[origin, to], q2.at[origin, r], o_send.at[origin, to], o_recv.at[origin, r], rows=to).start()
        q2[origin, r] = p2[origin, r]

    near = jnp.minimum(d, depth - 1 - d)

    def nth(step):
        value = step - near if step == 1 else step
        return jnp.where(2 * d < depth, value, depth - 1 - value)

    def relay(which, w, step, last=None):
        origin = nth(step)
        for part in (k, 1 - k):
            for way in range(2):
                @pl.when((origin < d) if way == 0 else (origin > d))
                def _():
                    copy = hop(which, w, origin, part, way)
                    copy.wait_recv()

                    @pl.when(can(way))
                    def _():
                        copy.start()

        if last is not None:
            for way, end in ((0, 0), (1, depth - 1)):
                @pl.when(origin == end)
                def _():
                    for part in (k, 1 - k):
                        start_hops(1, w1, part, (way,))
        return origin

    conv_two(d)

    for frm in range(chips):
        source = 2 * frm + c // 2

        @pl.when(source != r)
        def _():
            remote(s1.at[0, 0], r1.at[frm], f_send.at[0, 0], f_recv.at[frm], rows=source).wait_recv()

    for part in range(2):
        w1[d, part, :, 3 * half :] = jnp.zeros((3 * half, wide - 3 * half), bf16)
        for j in range(2):
            for side in range(3):
                at = side * half + j * GSIZE
                w1[d, part, :, at : at + GSIZE] = r1[2 * j + part, :, side * GSIZE : (side + 1) * GSIZE]

    for way, end in ((0, 0), (1, depth - 1)):
        @pl.when(d == end)
        def _():
            for part in (k, 1 - k):
                start_hops(1, w1, part, (way,))

    conv_two(relay(0, w2, 1, True))

    def activation(normed, gain, shift):
        linear = normed * gain + shift
        logistic = 1.0 / (1.0 + jnp.exp(-linear))
        return logistic * (1.0 + linear * (1.0 - logistic)) * gain

    wait_exchange(hid_s.at[0], hid_b, h_send, h_recv)
    plain = jnp.zeros((2 * GSIZE, lanes), f32)
    square = jnp.zeros((2 * GSIZE, lanes), f32)
    for h in range(rows):
        values = hid_b[h].astype(f32)
        plain += values
        square += values * values

    def two_means(values):
        per_lane = jnp.sum(values.reshape(2, GSIZE, lanes), axis=1)
        return image_totals(per_lane) * (1.0 / number)

    average2 = two_means(plain)
    inverse2 = lax.rsqrt(two_means(square) - average2 * average2 + 1e-05)
    inv2_ref[...] = inverse2
    for slot in range(2):
        at = pl.multiple_of((k + 2 * slot) * block + GSIZE * c, GSIZE)
        gain = par_ref[pl.ds(at, GSIZE), 2:3]
        shift = par_ref[pl.ds(at, GSIZE), 3:4]
        for h in range(rows):
            values = hid_b[h].astype(f32)[slot * GSIZE : (slot + 1) * GSIZE]
            normed = (values - average2[slot : slot + 1]) * inverse2[slot : slot + 1]
            spot = (h % 2) * GSIZE
            nrm2[slot, h // 2, spot : spot + GSIZE] = normed
            act2[slot, h // 2, spot : spot + GSIZE] = activation(normed, gain, shift)

    conv_two(relay(0, w2, 2, True))

    average1, meansq1 = wait_sums(0)
    inverse1 = lax.rsqrt(meansq1 - average1 * average1 + 1e-05)
    for g in range(groups):
        rows_g = pl.ds(g * GSIZE, GSIZE)
        normed = (nrm1[rows_g, :] - average1[g : g + 1]) * inverse1[g : g + 1]
        nrm1[rows_g, :] = normed
        act1[rows_g, :] = activation(normed, par_ref[rows_g, 0:1], par_ref[rows_g, 1:2])

    for step in range(3, depth):
        conv_two(relay(0, w2, step, True))

    for slot in range(2):
        for frm in range(chips):
            source = 2 * frm + c // 2

            @pl.when(source != r)
            def _():
                remote(
                    p1.at[0, 0], q1.at[slot, frm], p_send.at[0, 0], p_recv.at[slot, frm], rows=source
                ).wait_recv()

    hg = []
    for slot in range(2):
        sum_first = jnp.zeros((2 * GSIZE, lanes), f32)
        sum_second = jnp.zeros((2 * GSIZE, lanes), f32)
        scaled = []
        for m in range(rows // 2):
            total = q1[slot, 0, m].astype(f32)
            for frm in range(1, chips):
                total = total + q1[slot, frm, m].astype(f32)
            value = total * act2[slot, m]
            scaled.append(value)
            sum_first += value
            sum_second += value * nrm2[slot, m]
        first = image_totals(jnp.sum(sum_first, axis=0, keepdims=True)) * (1.0 / number)
        second = image_totals(jnp.sum(sum_second, axis=0, keepdims=True)) * (1.0 / number)
        inverse = inv2_ref[slot : slot + 1]
        hg.append([inverse * (scaled[m] - first - nrm2[slot, m] * second) for m in range(rows // 2)])
    for h in range(rows):
        spot = (h % 2) * GSIZE
        hg_s[h] = jnp.concatenate([hg[slot][h // 2][spot : spot + GSIZE] for slot in range(2)], axis=0).astype(bf16)
    swap = remote(hg_s, hg_r, b_send.at[1], b_recv.at[1], rows=sibling)
    swap.start()
    pending.append(swap)
    for h in range(rows):
        store_shifts(xs1, k, h, hg_s[h].astype(f32))
    swap.wait_recv()
    for h in range(rows):
        store_shifts(xs1, 1 - k, h, hg_r[h].astype(f32))

    conv_one(d)
    for step in range(1, depth):
        conv_one(relay(1, w1, step))

    for origin in range(depth):
        for off in range(1, rows):
            frm = lax.rem(r + off, rows)
            remote(
                p2.at[origin, frm], q2.at[origin, frm], o_send.at[origin, frm], o_recv.at[origin, frm], rows=frm
            ).wait_recv()

    one, two = [], []
    for origin in range(depth):
        for part in range(2):
            total = q2[origin, part].astype(f32)
            for frm in range(1, chips):
                total = total + q2[origin, 2 * frm + part].astype(f32)
            at = pl.ds(origin * block + part * half, half)
            value = total * act1[at, :]
            act1[at, :] = value
            one.append(jnp.sum(value.reshape(2, GSIZE, lanes), axis=1))
            two.append(jnp.sum((value * nrm1[at, :]).reshape(2, GSIZE, lanes), axis=1))
    send_sums(1, pack_sums(jnp.concatenate(one, axis=0), jnp.concatenate(two, axis=0)))
    first1, second1 = wait_sums(1)
    value = spread(inverse1) * (act1[...] - spread(first1) - nrm1[...] * spread(second1))
    out_ref[...] = (cot_t[...].astype(f32) + value).astype(bf16).T

    for copy in pending:
        copy.wait_send()
    for _ in each_shuffle(lambda copy: copy.wait_send()):
        pass
    for origin in range(depth):
        for _ in each_part(origin, lambda copy: copy.wait_send()):
            pass
        for off in range(1, rows):
            to = lax.rem(r + off, rows)
            remote(
                p2.at[origin, to], q2.at[origin, r], o_send.at[origin, to], o_recv.at[origin, r], rows=to
            ).wait_send()
    for which, w in ((0, w2), (1, w1)):
        for origin in range(depth):
            for part in range(2):
                for way in range(2):
                    @pl.when(can(way) & ((origin <= d) if way == 0 else (origin >= d)))
                    def _():
                        hop(which, w, origin, part, way).wait_send()


def kernel_body(
    depth, rows,
    latent, hidden, cotangent, filter_one, filter_two, gain_one, shift_one, gain_two, shift_two,
):
    images, _, breadth, channels = latent.shape
    lanes = images * breadth
    block = channels // depth
    half = block // 2
    chips = rows // 2
    wide = -(-3 * half // 128) * 128
    narrow = -(-3 * GSIZE // 128) * 128
    groups = channels // GSIZE
    bf16, f32 = jnp.bfloat16, jnp.float32
    dma = pltpu.SemaphoreType.DMA
    out = pl.pallas_call(
        functools.partial(kernel, depth, rows, breadth),
        out_shape=jax.ShapeDtypeStruct((lanes, channels), bf16),
        in_specs=[pl.BlockSpec(memory_space=pltpu.VMEM)] * 9,
        out_specs=pl.BlockSpec(memory_space=pltpu.VMEM),
        scratch_shapes=[
            pltpu.VMEM((channels, lanes), bf16),
            pltpu.VMEM((rows, block, lanes), bf16),
            pltpu.VMEM((rows, 2 * GSIZE, lanes), bf16),
            pltpu.VMEM((rows, 2 * GSIZE, lanes), bf16),
            pltpu.VMEM((depth, 2, 3 * half, wide), bf16),
            pltpu.VMEM((depth, 2, 3 * half, wide), bf16),
            pltpu.VMEM((2, 2, 3 * half, narrow), bf16),
            pltpu.VMEM((3 * half, wide), bf16),
            pltpu.VMEM((chips, 3 * half, narrow), bf16),
            pltpu.VMEM((2, rows, wide, lanes), bf16),
            pltpu.VMEM((2, rows, wide, lanes), bf16),
            pltpu.VMEM((rows, 3 * half, lanes), f32),
            pltpu.VMEM((depth, 2, rows // 2, 2 * GSIZE, lanes), bf16),
            pltpu.VMEM((2, chips, rows // 2, 2 * GSIZE, lanes), bf16),
            pltpu.VMEM((depth, rows, half, lanes), bf16),
            pltpu.VMEM((depth, rows, half, lanes), bf16),
            pltpu.VMEM((rows, 2 * GSIZE, lanes), bf16),
            pltpu.VMEM((rows, 2 * GSIZE, lanes), bf16),
            pltpu.VMEM((channels, lanes), f32),
            pltpu.VMEM((channels, lanes), f32),
            pltpu.VMEM((2, rows // 2, 2 * GSIZE, lanes), f32),
            pltpu.VMEM((2, rows // 2, 2 * GSIZE, lanes), f32),
            pltpu.VMEM((2, lanes), f32),
            pltpu.VMEM((2, groups, lanes), f32),
            pltpu.VMEM((2, rows, groups, lanes), f32),
            pltpu.VMEM((channels, 8), f32),
            dma((2, 2, depth, 2)), dma((2, depth, 2)),
            dma((2, 2)), dma((chips,)),
            dma((2,)), dma((2,)),
            dma((rows,)), dma((rows,)),
            dma((rows,)), dma((rows,)),
            dma((depth, 2)), dma((2, chips)),
            dma((2,)), dma((2,)),
            dma((depth, rows)), dma((depth, rows)),
            dma((2, rows)), dma((2, rows)),
        ],
        compiler_params=pltpu.CompilerParams(collective_id=0, has_side_effects=True),
    )(
        latent.reshape(lanes, channels), hidden.reshape(lanes, channels),
        cotangent.reshape(lanes, channels), filter_one, filter_two,
        gain_one, shift_one, gain_two, shift_two,
    )
    return out.reshape(latent.shape)


def solution(mesh):
    depth, rows = mesh.shape["dp"], mesh.shape["rows"]
    in_specs = (
        P("dp", "rows", None, None),
        P("dp", "rows", None, None),
        P("dp", "rows", None, None),
        P(None, "dp", "rows"),
        P(None, "dp", "rows"),
        P(),
        P(),
        P(),
        P(),
    )

    def body(latent, *rest):
        images, rows_here, breadth, channels = latent.shape
        fits = (
            rows_here == 1
            and images * breadth == 128
            and breadth % 4 == 0
            and depth == 4
            and rows == 2 * depth
            and channels == GROUPS * GSIZE
            and channels == depth * (rows // 2) * GSIZE
        )
        if fits:
            return kernel_body(depth, rows, latent, *rest)
        return plain_body(latent, *rest)

    return jax.shard_map(
        body, mesh=mesh, in_specs=in_specs, out_specs=P("dp", "rows", None, None), check_vma=False
    )
```

time: 58.7 us -> 57.7 us (0.983)
  Pallas kernels: 56.9 us -> 55.9 us
    pallas_call x1, Pallas kernels: 56.9 us -> 55.9 us  [kernel_body(): pl.pallas_call(functools.partial(kernel, depth, rows, breadth), out_shape...]
where the time goes in v1:
time: 57.7 us; the launch traced here: 57.5 us
  Pallas kernels  55.9 us (97%)
  local copies, waits for them, and re-layouts  1.6 us (3%)
    pallas_call x1, Pallas kernels, kernel_body(): pl.pallas_call(functools.partial(kernel, depth, rows, breadth), out_shape...  55.9 us
    unnamed x1, local copies, waits for them, and re-layouts  1.6 us

profile of v1, /device:TPU:0, one launch (start us, length us, event | category | flops | bytes accessed | tf_op | source)
XLA Modules:
  0.0 57.5 jit_solution(8262224706658189640)
XLA Ops:
  0.0 55.9 %shard_map.91 = bf16[128,640]{1,0:T(8,128)(2,1)} custom-call(bf16[128,640]{1,0:T(8,128)(2,1)} %bitcast.7, bf16[128,640]{1,0:T(8,128)(2,1)} %bitcast.8, bf16[128,640]{1,0:T(8,128)(2,1)} %bitcast.9, bf16[9,160,80]{2,1,0:T(8,128)(2,1)} %raw1.1, bf16[9,160,80]{2,1,0:T(8,128)(2,1)} %raw2.1, f32[640]{0:T(1024)} %gain1.1, f32[640]{0:T(1024)} %shift1.1, f32[640]{0:T(1024)} %gain2.1, ...), custom_call_target="tpu_custom_call" | custom-call | tf_op jit(solution)/shard_map/pallas_call | solution.py:564
  55.9 1.6 %copy.12 = bf16[2,1,64,640]{3,2,1,0:T(8,128)(2,1)} copy(bf16[2,1,64,640]{3,2,1,0:T(8,128)(2,1)} %bitcast.6) | data formatting | bytes 327680

commit v2 on v1

--- a/solution.py
+++ b/solution.py
@@ -100,13 +100,14 @@
 
 def kernel(
     depth, rows, breadth,
-    lat_ref, hid_ref, cot_ref, raw1, raw2, gain1, shift1, gain2, shift2,
+    lat_hbm, hid_hbm, cot_hbm, raw1_hbm, raw2_hbm, gain1_hbm, shift1_hbm, gain2_hbm, shift2_hbm,
     out_ref,
+    lat_ref, hid_ref, cot_ref, raw1, raw2, gain1, shift1, gain2, shift2, in_sem,
     cot_t, x_cot, hid_s, hid_b, w1, w2, s1, s2, r1,
     xs1, xs2, y_ref, p1, q1, p2, q2, hg_s, hg_r,
     nrm1, act1, nrm2, act2, inv2_ref, st_s, st_b, par_ref,
     z_send, z_recv, f_send, f_recv, b_send, b_recv, c_send, c_recv, h_send, h_recv,
-    p_send, p_recv, g_send, g_recv, o_send, o_recv, t_send, t_recv,
+    p_send, p_recv, o_send, o_recv, t_send, t_recv,
 ):
     d = lax.axis_index("dp")
     r = lax.axis_index("rows")
@@ -143,11 +144,33 @@
         pl.semaphore_signal(barrier, inc=1, device_id={"rows": lax.rem(r + off, rows)}, device_id_type=MESH)
 
     pending = []
+    loads = {
+        name: pltpu.make_async_copy(src, dst, in_sem.at[index])
+        for index, (name, src, dst) in enumerate((
+            ("raw2", raw2_hbm, raw2), ("cot", cot_hbm, cot_ref), ("hid", hid_hbm, hid_ref),
+            ("raw1", raw1_hbm, raw1), ("lat", lat_hbm, lat_ref), ("gain1", gain1_hbm, gain1),
+            ("shift1", shift1_hbm, shift1), ("gain2", gain2_hbm, gain2), ("shift2", shift2_hbm, shift2),
+        ))
+    }
+    for load in loads.values():
+        load.start()
+
+    pad = wide - 3 * half
+    own = k == c // 2
+    w2[d, k, :, 3 * half :] = jnp.zeros((3 * half, pad), bf16)
+    s2[:, 3 * half :] = jnp.zeros((3 * half, pad), bf16)
+    for part in range(2):
+        w1[d, part, :, 3 * half :] = jnp.zeros((3 * half, pad), bf16)
+        for side_core in range(2):
+            s1[part, side_core, :, 3 * GSIZE :] = jnp.zeros((3 * half, s1.shape[3] - 3 * GSIZE), bf16)
+    for xs in (xs1, xs2):
+        for part in range(2):
+            for h in range(rows):
+                xs[part, h, 3 * half :] = jnp.zeros((pad, lanes), bf16)
+    loads["raw2"].wait()
 
     def arrange(ready, raw, which):
         start = pl.multiple_of(which * half, 16)
-        pad = wide - 3 * half
-        ready[:, 3 * half :] = jnp.zeros((3 * half, pad), bf16)
         for tap in range(TAPS):
             down, side = tap // 3, tap % 3
             ready[down * half : (down + 1) * half, side * half : (side + 1) * half] = raw[
@@ -160,26 +183,67 @@
     beside = jnp.where((d > 0) & (d < depth - 1), 2, 1)
     pl.semaphore_wait(barrier, rows - 1 + beside)
 
-    def hop(which, w, origin, part, way):
+    segments = ((0, 128), (128, 3 * half))
+
+    def hop(which, w, origin, part, seg, way):
+        low, high = segments[seg]
+        piece = w.at[origin, part, low:high]
         return remote(
-            w.at[origin, part], w.at[origin, part],
-            z_send.at[which, way, origin, part], z_recv.at[which, origin, part], dp=d + 1 - 2 * way,
+            piece, piece, z_send.at[which, way], z_recv.at[which, origin, part, seg], dp=d + 1 - 2 * way
         )
 
-    def can(way):
-        return (d < depth - 1) if way == 0 else (d > 0)
+    middle = (d > 0) & (d < depth - 1)
+    near = jnp.minimum(d, depth - 1 - d)
+
+    def nth(step):
+        value = step - near if step == 1 else step
+        return jnp.where(2 * d < depth, value, depth - 1 - value)
 
     def start_hops(which, w, part, ways=(0, 1)):
         for way in ways:
-            @pl.when(can(way))
+            @pl.when((d < depth - 1) if way == 0 else (d > 0))
             def _():
-                hop(which, w, d, part, way).start()
+                for seg in range(2):
+                    hop(which, w, d, part, seg, way).start()
+
+    def forward(which, w, step, index):
+        origin = nth(step)
+        part, seg = (k, 1 - k)[index // 2], index % 2
+        for way in range(2):
+            @pl.when(middle & ((origin < d) if way == 0 else (origin > d)))
+            def _():
+                copy = hop(which, w, origin, part, seg, way)
+                copy.wait_recv()
+                copy.start()
+
+    def take(which, w, step):
+        origin = nth(step)
+
+        @pl.when(jnp.logical_not(middle))
+        def _():
+            for part in (k, 1 - k):
+                for seg in range(2):
+                    hop(which, w, origin, part, seg, 0).wait_recv()
+
+        return origin
+
+    def wait_hops(which, w):
+        for here in range(depth):
+            for way, low, high in ((0, 0, here + 1), (1, here, depth)):
+                if (way == 0 and here < depth - 1) or (way == 1 and here > 0):
+                    @pl.when(d == here)
+                    def _():
+                        span = w.at[low:high]
+                        remote(
+                            span, span, z_send.at[which, way], z_recv.at[which, 0, 0, 0], dp=d + 1 - 2 * way
+                        ).wait_send()
 
     start_hops(0, w2, k)
     twin = remote(s2, w2.at[d, k], b_send.at[0], b_recv.at[0], rows=sibling)
     twin.start()
     pending.append(twin)
 
+    loads["cot"].wait()
     cot_t[...] = cot_ref[...].T
 
     def piece_of(to):
@@ -187,14 +251,10 @@
 
     for off in range(1, rows):
         to = lax.rem(r + off, rows)
-        copy = remote(piece_of(to), x_cot.at[r], c_send.at[to], c_recv.at[r], rows=to)
-        copy.start()
-        pending.append(copy)
+        remote(piece_of(to), x_cot.at[r], c_send.at[0], c_recv.at[0], rows=to).start()
     x_cot[r] = piece_of(r)[...]
 
-    remote(s2, w2.at[d, 1 - k], b_send.at[0], b_recv.at[0], rows=sibling).wait_recv()
-    start_hops(0, w2, 1 - k)
-
+    loads["hid"].wait()
     hid_full = hid_ref[...].astype(f32).T
     for to in range(rows):
         parts = [
@@ -204,42 +264,41 @@
         hid_s[to] = jnp.concatenate(parts, axis=0).astype(bf16)
     for off in range(1, rows):
         to = lax.rem(r + off, rows)
-        copy = remote(hid_s.at[to], hid_b.at[r], h_send.at[to], h_recv.at[r], rows=to)
-        copy.start()
-        pending.append(copy)
+        remote(hid_s.at[to], hid_b.at[r], h_send.at[0], h_recv.at[0], rows=to).start()
     hid_b[r] = hid_s[r]
 
+    remote(s2, w2.at[d, 1 - k], b_send.at[0], b_recv.at[0], rows=sibling).wait_recv()
+    start_hops(0, w2, 1 - k)
+
+    loads["raw1"].wait()
     for part in range(2):
         for side_core in range(2):
             ready = s1.at[part, side_core]
-            ready[:, 3 * GSIZE :] = jnp.zeros((3 * half, ready.shape[1] - 3 * GSIZE), bf16)
             for tap in range(TAPS):
                 down, side = tap // 3, tap % 3
                 ready[down * half : (down + 1) * half, side * GSIZE : (side + 1) * GSIZE] = raw1[
                     tap, side_core * half : (side_core + 1) * half, part * GSIZE : (part + 1) * GSIZE
                 ]
 
-    def each_shuffle(act):
-        for part in range(2):
-            for side_core in range(2):
-                to = 2 * (2 * k + part) + side_core
-                src = s1.at[part, side_core]
-
-                @pl.when(to != r)
-                def _():
-                    act(remote(src, r1.at[c], f_send.at[part, side_core], f_recv.at[c], rows=to))
-
-                yield to, src
-
-    for to, src in each_shuffle(lambda copy: copy.start()):
-        @pl.when(to == r)
-        def _():
-            r1[c] = src[...]
-
+    for part in range(2):
+        for side_core in range(2):
+            to = 2 * (2 * k + part) + side_core
+
+            @pl.when(to != r)
+            def _():
+                remote(s1.at[part, side_core], r1.at[c], f_send.at[0], f_recv.at[0], rows=to).start()
+
+            @pl.when(to == r)
+            def _():
+                r1[c] = s1[part, side_core]
+
+    forward(0, w2, 1, 0)
+    forward(0, w2, 2, 0)
+    loads["lat"].wait()
     lane = lax.broadcasted_iota(jnp.int32, (1, lanes), 1)
     column = lax.rem(lane, breadth)
     image_of = lax.div(lane, breadth)
-    first_half = lax.rem(lane, breadth) < breadth // 2
+    quarter = lax.rem(lane, breadth) // (breadth // 4)
 
     def image_totals(per_lane):
         total = jnp.zeros_like(per_lane)
@@ -250,33 +309,32 @@
         return total
 
     def pack_sums(one, two):
-        return jnp.where(first_half, image_totals(one), image_totals(two))
+        one, two = image_totals(one), image_totals(two)
+        top, low = slice(0, groups // 2), slice(groups // 2, groups)
+        return jnp.where(
+            quarter == 0, one[top], jnp.where(quarter == 1, two[top], jnp.where(quarter == 2, one[low], two[low]))
+        )
 
     def send_sums(which, packed):
         st_s[which] = packed
         for off in range(1, rows):
             to = lax.rem(r + off, rows)
-            copy = remote(st_s.at[which], st_b.at[which, r], t_send.at[which, to], t_recv.at[which, r], rows=to)
-            copy.start()
-            pending.append(copy)
+            remote(st_s.at[which], st_b.at[which, r], t_send.at[which], t_recv.at[which], rows=to).start()
         st_b[which, r] = packed
 
     def wait_sums(which):
-        for off in range(1, rows):
-            frm = lax.rem(r + off, rows)
-            remote(
-                st_s.at[which], st_b.at[which, frm], t_send.at[which, frm], t_recv.at[which, frm], rows=frm
-            ).wait_recv()
+        span = st_b.at[which, 0 : rows - 1]
+        remote(span, span, t_send.at[which], t_recv.at[which], rows=sibling).wait_recv()
         total = st_b[which, 0]
         for h in range(1, rows):
             total = total + st_b[which, h]
         total = total * (1.0 / number)
-        quarter = breadth // 2
-        ahead = pltpu.roll(total, lanes - quarter, 1)
-        behind = pltpu.roll(total, quarter, 1)
-        one = jnp.where(first_half, total, behind)
-        two = jnp.where(first_half, ahead, total)
-        return one, two
+        full = []
+        for at in range(4):
+            mine = jnp.where(quarter == at, total, 0.0)
+            pair = mine + pltpu.roll(mine, ((1 if at % 2 == 0 else -1) * breadth // 4) % lanes, 1)
+            full.append(pair + pltpu.roll(pair, ((1 if at < 2 else -1) * breadth // 2) % lanes, 1))
+        return jnp.concatenate([full[0], full[2]], axis=0), jnp.concatenate([full[1], full[3]], axis=0)
 
     def spread(moment):
         return jnp.broadcast_to(moment[:, None, :], (groups, GSIZE, lanes)).reshape(channels, lanes)
@@ -287,6 +345,8 @@
     nrm1[...] = lat_ref[...].astype(f32).T
     send_sums(0, pack_sums(by_group(nrm1[...]), by_group(nrm1[...] * nrm1[...])))
 
+    for name in ("gain1", "shift1", "gain2", "shift2"):
+        loads[name].wait()
     raw_params = [p[...].reshape(1, channels) for p in (gain1, shift1, gain2, shift2)]
     par_ref[...] = jnp.concatenate(raw_params + raw_params, axis=0).T
 
@@ -297,17 +357,13 @@
         xs[part, h, half : 2 * half] = values.astype(bf16)
         xs[part, h, 2 * half : 3 * half] = right.astype(bf16)
 
-    for xs in (xs1, xs2):
-        for part in range(2):
-            for h in range(rows):
-                xs[part, h, 3 * half :] = jnp.zeros((wide - 3 * half, lanes), bf16)
-
-    def wait_exchange(src, dst, send, recv):
-        for off in range(1, rows):
-            frm = lax.rem(r + off, rows)
-            remote(src, dst.at[frm], send.at[frm], recv.at[frm], rows=frm).wait_recv()
-
-    wait_exchange(piece_of(r), x_cot, c_send, c_recv)
+    def wait_group(src, dst, send, recv):
+        remote(src, dst, send, recv, rows=sibling).wait_recv()
+
+    forward(0, w2, 1, 1)
+    forward(0, w2, 2, 1)
+    everyone = x_cot.at[0 : rows - 1]
+    wait_group(everyone, everyone, c_send.at[0], c_recv.at[0])
     for h in range(rows):
         values = x_cot[h].astype(f32)
         for part in range(2):
@@ -331,19 +387,6 @@
             total = total + y_ref[h - 1, 2 * half : 3 * half]
         return total
 
-    def each_part(origin, act):
-        for j in range(2):
-            to = 2 * (2 * k + j) + lax.rem(origin, 2)
-            slot = origin // 2
-
-            @pl.when(to != r)
-            def _():
-                act(remote(
-                    p1.at[origin, j], q1.at[slot, c], p_send.at[origin, j], p_recv.at[slot, c], rows=to
-                ))
-
-            yield j, to, slot
-
     def conv_two(origin):
         conv(w2, origin, xs2)
         for h in range(0, rows, 2):
@@ -351,7 +394,14 @@
             for j in range(2):
                 both = [low[j * GSIZE : (j + 1) * GSIZE], high[j * GSIZE : (j + 1) * GSIZE]]
                 p1[origin, j, h // 2] = jnp.concatenate(both, axis=0).astype(bf16)
-        for j, to, slot in each_part(origin, lambda copy: copy.start()):
+        slot = origin // 2
+        for j in range(2):
+            to = 2 * (2 * k + j) + lax.rem(origin, 2)
+
+            @pl.when(to != r)
+            def _():
+                remote(p1.at[origin, j], q1.at[slot, c], p_send.at[0], p_recv.at[slot], rows=to).start()
+
             @pl.when(to == r)
             def _():
                 q1[slot, c] = p1[origin, j]
@@ -362,66 +412,24 @@
             p2[origin, h] = row_of(h).astype(bf16)
         for off in range(1, rows):
             to = lax.rem(r + off, rows)
-            remote(p2.at[origin, to], q2.at[origin, r], o_send.at[origin, to], o_recv.at[origin, r], rows=to).start()
+            remote(p2.at[origin, to], q2.at[origin, r], o_send.at[0], o_recv.at[origin], rows=to).start()
         q2[origin, r] = p2[origin, r]
 
-    near = jnp.minimum(d, depth - 1 - d)
-
-    def nth(step):
-        value = step - near if step == 1 else step
-        return jnp.where(2 * d < depth, value, depth - 1 - value)
-
-    def relay(which, w, step, last=None):
-        origin = nth(step)
-        for part in (k, 1 - k):
-            for way in range(2):
-                @pl.when((origin < d) if way == 0 else (origin > d))
-                def _():
-                    copy = hop(which, w, origin, part, way)
-                    copy.wait_recv()
-
-                    @pl.when(can(way))
-                    def _():
-                        copy.start()
-
-        if last is not None:
-            for way, end in ((0, 0), (1, depth - 1)):
-                @pl.when(origin == end)
-                def _():
-                    for part in (k, 1 - k):
-                        start_hops(1, w1, part, (way,))
-        return origin
-
+    forward(0, w2, 1, 2)
+    forward(0, w2, 2, 2)
     conv_two(d)
-
-    for frm in range(chips):
-        source = 2 * frm + c // 2
-
-        @pl.when(source != r)
-        def _():
-            remote(s1.at[0, 0], r1.at[frm], f_send.at[0, 0], f_recv.at[frm], rows=source).wait_recv()
-
-    for part in range(2):
-        w1[d, part, :, 3 * half :] = jnp.zeros((3 * half, wide - 3 * half), bf16)
-        for j in range(2):
-            for side in range(3):
-                at = side * half + j * GSIZE
-                w1[d, part, :, at : at + GSIZE] = r1[2 * j + part, :, side * GSIZE : (side + 1) * GSIZE]
-
-    for way, end in ((0, 0), (1, depth - 1)):
-        @pl.when(d == end)
-        def _():
-            for part in (k, 1 - k):
-                start_hops(1, w1, part, (way,))
-
-    conv_two(relay(0, w2, 1, True))
+    forward(0, w2, 1, 3)
+    forward(0, w2, 2, 3)
+    take(0, w2, 1)
+    conv_two(nth(1))
 
     def activation(normed, gain, shift):
         linear = normed * gain + shift
         logistic = 1.0 / (1.0 + jnp.exp(-linear))
         return logistic * (1.0 + linear * (1.0 - logistic)) * gain
 
-    wait_exchange(hid_s.at[0], hid_b, h_send, h_recv)
+    everyone = hid_b.at[0 : rows - 1]
+    wait_group(everyone, everyone, h_send.at[0], h_recv.at[0])
     plain = jnp.zeros((2 * GSIZE, lanes), f32)
     square = jnp.zeros((2 * GSIZE, lanes), f32)
     for h in range(rows):
@@ -447,7 +455,38 @@
             nrm2[slot, h // 2, spot : spot + GSIZE] = normed
             act2[slot, h // 2, spot : spot + GSIZE] = activation(normed, gain, shift)
 
-    conv_two(relay(0, w2, 2, True))
+    forward(0, w2, 3, 0)
+    for count, here in ((chips - 1, own), (chips, jnp.logical_not(own))):
+        @pl.when(here)
+        def _():
+            span = r1.at[0:count]
+            wait_group(span, span, f_send.at[0], f_recv.at[0])
+
+    for part in range(2):
+        for j in range(2):
+            for side in range(3):
+                at = side * half + j * GSIZE
+                w1[d, part, :, at : at + GSIZE] = r1[2 * j + part, :, side * GSIZE : (side + 1) * GSIZE]
+
+    for way, here in ((0, 2 * d < depth), (1, 2 * d >= depth)):
+        @pl.when(here)
+        def _():
+            for part in (k, 1 - k):
+                start_hops(1, w1, part, (way,))
+
+    forward(0, w2, 3, 1)
+    take(0, w2, 2)
+    conv_two(nth(2))
+    forward(0, w2, 3, 2)
+    forward(0, w2, 3, 3)
+    for way, here in ((0, 2 * d >= depth), (1, 2 * d < depth)):
+        @pl.when(here)
+        def _():
+            for part in (k, 1 - k):
+                start_hops(1, w1, part, (way,))
+
+    take(0, w2, 3)
+    conv_two(nth(3))
 
     average1, meansq1 = wait_sums(0)
     inverse1 = lax.rsqrt(meansq1 - average1 * average1 + 1e-05)
@@ -457,18 +496,16 @@
         nrm1[rows_g, :] = normed
         act1[rows_g, :] = activation(normed, par_ref[rows_g, 0:1], par_ref[rows_g, 1:2])
 
-    for step in range(3, depth):
-        conv_two(relay(0, w2, step, True))
-
-    for slot in range(2):
-        for frm in range(chips):
-            source = 2 * frm + c // 2
-
-            @pl.when(source != r)
-            def _():
-                remote(
-                    p1.at[0, 0], q1.at[slot, frm], p_send.at[0, 0], p_recv.at[slot, frm], rows=source
-                ).wait_recv()
+    for index in range(4):
+        forward(1, w1, 1, index)
+        forward(1, w1, 2, index)
+
+    for count, here in ((chips - 1, own), (chips, jnp.logical_not(own))):
+        @pl.when(here)
+        def _():
+            for slot in range(2):
+                span = q1.at[slot, 0:count]
+                wait_group(span, span, p_send.at[0], p_recv.at[slot])
 
     hg = []
     for slot in range(2):
@@ -499,16 +536,20 @@
     for h in range(rows):
         store_shifts(xs1, 1 - k, h, hg_r[h].astype(f32))
 
+    forward(1, w1, 3, 0)
     conv_one(d)
-    for step in range(1, depth):
-        conv_one(relay(1, w1, step))
-
+    forward(1, w1, 3, 1)
+    take(1, w1, 1)
+    conv_one(nth(1))
+    forward(1, w1, 3, 2)
+    take(1, w1, 2)
+    conv_one(nth(2))
+    forward(1, w1, 3, 3)
+    take(1, w1, 3)
+    conv_one(nth(3))
     for origin in range(depth):
-        for off in range(1, rows):
-            frm = lax.rem(r + off, rows)
-            remote(
-                p2.at[origin, frm], q2.at[origin, frm], o_send.at[origin, frm], o_recv.at[origin, frm], rows=frm
-            ).wait_recv()
+        span = q2.at[origin, 0 : rows - 1]
+        wait_group(span, span, o_send.at[0], o_recv.at[origin])
 
     one, two = [], []
     for origin in range(depth):
@@ -528,23 +569,22 @@
 
     for copy in pending:
         copy.wait_send()
-    for _ in each_shuffle(lambda copy: copy.wait_send()):
-        pass
-    for origin in range(depth):
-        for _ in each_part(origin, lambda copy: copy.wait_send()):
-            pass
-        for off in range(1, rows):
-            to = lax.rem(r + off, rows)
-            remote(
-                p2.at[origin, to], q2.at[origin, r], o_send.at[origin, to], o_recv.at[origin, r], rows=to
-            ).wait_send()
-    for which, w in ((0, w2), (1, w1)):
-        for origin in range(depth):
-            for part in range(2):
-                for way in range(2):
-                    @pl.when(can(way) & ((origin <= d) if way == 0 else (origin >= d)))
-                    def _():
-                        hop(which, w, origin, part, way).wait_send()
+    def sent(span, send, recv):
+        remote(span, span, send, recv, rows=sibling).wait_send()
+
+    sent(x_cot.at[0 : rows - 1], c_send.at[0], c_recv.at[0])
+    sent(hid_b.at[0 : rows - 1], h_send.at[0], h_recv.at[0])
+    for which in range(2):
+        sent(st_b.at[which, 0 : rows - 1], t_send.at[which], t_recv.at[which])
+    sent(p2.at[:, 0 : rows - 1], o_send.at[0], o_recv.at[0])
+    for count, here in ((chips - 1, own), (chips, jnp.logical_not(own))):
+        @pl.when(here)
+        def _():
+            sent(r1.at[0:count], f_send.at[0], f_recv.at[0])
+            sent(q1.at[:, 0:count], p_send.at[0], p_recv.at[0])
+
+    wait_hops(0, w2)
+    wait_hops(1, w1)
 
 
 def kernel_body(
@@ -564,9 +604,19 @@
     out = pl.pallas_call(
         functools.partial(kernel, depth, rows, breadth),
         out_shape=jax.ShapeDtypeStruct((lanes, channels), bf16),
-        in_specs=[pl.BlockSpec(memory_space=pltpu.VMEM)] * 9,
+        in_specs=[pl.BlockSpec(memory_space=pltpu.HBM)] * 9,
         out_specs=pl.BlockSpec(memory_space=pltpu.VMEM),
         scratch_shapes=[
+            pltpu.VMEM((lanes, channels), bf16),
+            pltpu.VMEM((lanes, channels), bf16),
+            pltpu.VMEM((lanes, channels), bf16),
+            pltpu.VMEM(filter_one.shape, bf16),
+            pltpu.VMEM(filter_two.shape, bf16),
+            pltpu.VMEM((channels,), f32),
+            pltpu.VMEM((channels,), f32),
+            pltpu.VMEM((channels,), f32),
+            pltpu.VMEM((channels,), f32),
+            dma((9,)),
             pltpu.VMEM((channels, lanes), bf16),
             pltpu.VMEM((rows, block, lanes), bf16),
             pltpu.VMEM((rows, 2 * GSIZE, lanes), bf16),
@@ -590,20 +640,21 @@
             pltpu.VMEM((2, rows // 2, 2 * GSIZE, lanes), f32),
             pltpu.VMEM((2, rows // 2, 2 * GSIZE, lanes), f32),
             pltpu.VMEM((2, lanes), f32),
-            pltpu.VMEM((2, groups, lanes), f32),
-            pltpu.VMEM((2, rows, groups, lanes), f32),
+            pltpu.VMEM((2, groups // 2, lanes), f32),
+            pltpu.VMEM((2, rows, groups // 2, lanes), f32),
             pltpu.VMEM((channels, 8), f32),
-            dma((2, 2, depth, 2)), dma((2, depth, 2)),
-            dma((2, 2)), dma((chips,)),
+            dma((2, 2)), dma((2, depth, 2, 2)),
+            dma((1,)), dma((1,)),
             dma((2,)), dma((2,)),
-            dma((rows,)), dma((rows,)),
-            dma((rows,)), dma((rows,)),
-            dma((depth, 2)), dma((2, chips)),
+            dma((1,)), dma((1,)),
+            dma((1,)), dma((1,)),
+            dma((1,)), dma((2,)),
+            dma((1,)), dma((depth,)),
             dma((2,)), dma((2,)),
-            dma((depth, rows)), dma((depth, rows)),
-            dma((2, rows)), dma((2, rows)),
         ],
-        compiler_params=pltpu.CompilerParams(collective_id=0, has_side_effects=True),
+        compiler_params=pltpu.CompilerParams(
+            collective_id=0, has_side_effects=True
+        ),
     )(
         latent.reshape(lanes, channels), hidden.reshape(lanes, channels),
         cotangent.reshape(lanes, channels), filter_one, filter_two,

time: 57.7 us -> 48.7 us (0.84)
  Pallas kernels: 55.9 us -> 47 us
    pallas_call x1, Pallas kernels: 55.9 us -> 47 us  [kernel_body(): pl.pallas_call(functools.partial(kernel, depth, rows, breadth), out_shape...]
where the time goes in v2:
time: 48.7 us; the launch traced here: 48.6 us
  Pallas kernels  47 us (97%)
  local copies, waits for them, and re-layouts  1.6 us (3%)
    pallas_call x1, Pallas kernels, kernel_body(): pl.pallas_call(functools.partial(kernel, depth, rows, breadth), out_shape...  47 us
    unnamed x1, local copies, waits for them, and re-layouts  1.6 us

profile of v2, /device:TPU:0, one launch (start us, length us, event | category | flops | bytes accessed | tf_op | source)
XLA Modules:
  0.0 48.6 jit_solution(3230170480898288618)
XLA Ops:
  0.0 47.0 %shard_map.91 = bf16[128,640]{1,0:T(8,128)(2,1)} custom-call(bf16[128,640]{1,0:T(8,128)(2,1)} %bitcast.7, bf16[128,640]{1,0:T(8,128)(2,1)} %bitcast.8, bf16[128,640]{1,0:T(8,128)(2,1)} %bitcast.9, bf16[9,160,80]{2,1,0:T(8,128)(2,1)} %raw1_hbm.1, bf16[9,160,80]{2,1,0:T(8,128)(2,1)} %raw2_hbm.1, f32[640]{0:T(1024)} %gain1_hbm.1, f32[640]{0:T(1024)} %shift1_hbm.1, ...), custom_call_target="tpu_custom_call" | custom-call | tf_op jit(solution)/shard_map/pallas_call | solution.py:604
  47.0 1.6 %copy.12 = bf16[2,1,64,640]{3,2,1,0:T(8,128)(2,1)} copy(bf16[2,1,64,640]{3,2,1,0:T(8,128)(2,1)} %bitcast.6) | data formatting | bytes 327680

commit v3 on v2

--- a/solution.py
+++ b/solution.py
@@ -103,11 +103,12 @@
     lat_hbm, hid_hbm, cot_hbm, raw1_hbm, raw2_hbm, gain1_hbm, shift1_hbm, gain2_hbm, shift2_hbm,
     out_ref,
     lat_ref, hid_ref, cot_ref, raw1, raw2, gain1, shift1, gain2, shift2, in_sem,
-    cot_t, x_cot, hid_s, hid_b, w1, w2, s1, s2, r1,
+    cot_t, x_cot, hid_b, w1, w2, s1, s2, r1,
     xs1, xs2, y_ref, p1, q1, p2, q2, hg_s, hg_r,
     nrm1, act1, nrm2, act2, inv2_ref, st_s, st_b, par_ref,
+    x_far, hid_two, hid_far, xs_far, p_far, q_far, nrm_far, act_far, hg_far, hg_two,
     z_send, z_recv, f_send, f_recv, b_send, b_recv, c_send, c_recv, h_send, h_recv,
-    p_send, p_recv, o_send, o_recv, t_send, t_recv,
+    p_send, p_recv, o_send, o_recv, t_send, t_recv, d_send, d_recv, e_send, e_recv,
 ):
     d = lax.axis_index("dp")
     r = lax.axis_index("rows")
@@ -132,13 +133,16 @@
 
     barrier = pltpu.get_barrier_semaphore()
 
-    @pl.when(d > 0)
-    def _():
-        pl.semaphore_signal(barrier, inc=1, device_id={"dp": d - 1}, device_id_type=MESH)
-
-    @pl.when(d < depth - 1)
-    def _():
-        pl.semaphore_signal(barrier, inc=1, device_id={"dp": d + 1}, device_id_type=MESH)
+    middle = (d > 0) & (d < depth - 1)
+    partner = d + 1 - 2 * lax.rem(d, 2)
+    lent = jnp.where(2 * d < depth, 1, 0)
+
+    @pl.when(middle)
+    def _():
+        pl.semaphore_signal(barrier, inc=1, device_id={"dp": depth - 1 - d}, device_id_type=MESH)
+
+    for to in range(rows):
+        pl.semaphore_signal(barrier, inc=1, device_id={"dp": partner, "rows": to}, device_id_type=MESH)
 
     for off in range(1, rows):
         pl.semaphore_signal(barrier, inc=1, device_id={"rows": lax.rem(r + off, rows)}, device_id_type=MESH)
@@ -163,7 +167,7 @@
         w1[d, part, :, 3 * half :] = jnp.zeros((3 * half, pad), bf16)
         for side_core in range(2):
             s1[part, side_core, :, 3 * GSIZE :] = jnp.zeros((3 * half, s1.shape[3] - 3 * GSIZE), bf16)
-    for xs in (xs1, xs2):
+    for xs in (xs1, xs2, xs_far):
         for part in range(2):
             for h in range(rows):
                 xs[part, h, 3 * half :] = jnp.zeros((pad, lanes), bf16)
@@ -180,8 +184,7 @@
     arrange(w2.at[d, k], raw2, k)
     arrange(s2, raw2, 1 - k)
 
-    beside = jnp.where((d > 0) & (d < depth - 1), 2, 1)
-    pl.semaphore_wait(barrier, rows - 1 + beside)
+    pl.semaphore_wait(barrier, 2 * rows - 1 + jnp.where(middle, 1, 0))
 
     segments = ((0, 128), (128, 3 * half))
 
@@ -192,7 +195,6 @@
             piece, piece, z_send.at[which, way], z_recv.at[which, origin, part, seg], dp=d + 1 - 2 * way
         )
 
-    middle = (d > 0) & (d < depth - 1)
     near = jnp.minimum(d, depth - 1 - d)
 
     def nth(step):
@@ -217,26 +219,23 @@
                 copy.start()
 
     def take(which, w, step):
-        origin = nth(step)
-
+        for part in (k, 1 - k):
+            for seg in range(2):
+                hop(which, w, nth(step), part, seg, 0).wait_recv()
+
+    def take_end(which, w, step):
         @pl.when(jnp.logical_not(middle))
         def _():
-            for part in (k, 1 - k):
-                for seg in range(2):
-                    hop(which, w, origin, part, seg, 0).wait_recv()
-
-        return origin
-
-    def wait_hops(which, w):
-        for here in range(depth):
-            for way, low, high in ((0, 0, here + 1), (1, here, depth)):
-                if (way == 0 and here < depth - 1) or (way == 1 and here > 0):
-                    @pl.when(d == here)
-                    def _():
-                        span = w.at[low:high]
-                        remote(
-                            span, span, z_send.at[which, way], z_recv.at[which, 0, 0, 0], dp=d + 1 - 2 * way
-                        ).wait_send()
+            take(which, w, step)
+
+    def wait_hops(which, w, spans):
+        for here, way, low, high in spans:
+            @pl.when(d == here)
+            def _():
+                span = w.at[low:high]
+                remote(
+                    span, span, z_send.at[which, way], z_recv.at[which, 0, 0, 0], dp=d + 1 - 2 * way
+                ).wait_send()
 
     start_hops(0, w2, k)
     twin = remote(s2, w2.at[d, k], b_send.at[0], b_recv.at[0], rows=sibling)
@@ -249,26 +248,10 @@
     def piece_of(to):
         return cot_t.at[pl.ds(pl.multiple_of((to // 2) * block, block), block), :]
 
-    for off in range(1, rows):
-        to = lax.rem(r + off, rows)
-        remote(piece_of(to), x_cot.at[r], c_send.at[0], c_recv.at[0], rows=to).start()
-    x_cot[r] = piece_of(r)[...]
-
-    loads["hid"].wait()
-    hid_full = hid_ref[...].astype(f32).T
-    for to in range(rows):
-        parts = [
-            hid_full[block * b + GSIZE * (to // 2) : block * b + GSIZE * (to // 2 + 1)]
-            for b in (to % 2, to % 2 + 2)
-        ]
-        hid_s[to] = jnp.concatenate(parts, axis=0).astype(bf16)
-    for off in range(1, rows):
-        to = lax.rem(r + off, rows)
-        remote(hid_s.at[to], hid_b.at[r], h_send.at[0], h_recv.at[0], rows=to).start()
-    hid_b[r] = hid_s[r]
-
-    remote(s2, w2.at[d, 1 - k], b_send.at[0], b_recv.at[0], rows=sibling).wait_recv()
-    start_hops(0, w2, 1 - k)
+    for off in range(1, chips):
+        to = 2 * lax.rem(c + off, chips) + k
+        remote(piece_of(to), x_cot.at[k, c], c_send.at[0], c_recv.at[0], rows=to).start()
+    x_cot[k, c] = piece_of(r)[...]
 
     loads["raw1"].wait()
     for part in range(2):
@@ -292,8 +275,24 @@
             def _():
                 r1[c] = s1[part, side_core]
 
+    loads["hid"].wait()
+    hid_full = hid_ref[...].astype(f32).T
+    for to in range(rows):
+        parts = [
+            hid_full[block * b + GSIZE * (to // 2) : block * b + GSIZE * (to // 2 + 1)]
+            for b in (to % 2, to % 2 + 2)
+        ]
+        for slot in range(2):
+            hid_two[to, slot] = parts[slot].astype(bf16)
+    for off in range(1, rows):
+        to = lax.rem(r + off, rows)
+        remote(hid_two.at[to], hid_b.at[:, r], h_send.at[0], h_recv.at[0], rows=to).start()
+    hid_b[:, r] = hid_two[r]
+
+    remote(s2, w2.at[d, 1 - k], b_send.at[0], b_recv.at[0], rows=sibling).wait_recv()
+    start_hops(0, w2, 1 - k)
+
     forward(0, w2, 1, 0)
-    forward(0, w2, 2, 0)
     loads["lat"].wait()
     lane = lax.broadcasted_iota(jnp.int32, (1, lanes), 1)
     column = lax.rem(lane, breadth)
@@ -361,13 +360,29 @@
         remote(src, dst, send, recv, rows=sibling).wait_recv()
 
     forward(0, w2, 1, 1)
-    forward(0, w2, 2, 1)
-    everyone = x_cot.at[0 : rows - 1]
+    everyone = x_cot.at[0, 0 : chips - 1]
     wait_group(everyone, everyone, c_send.at[0], c_recv.at[0])
-    for h in range(rows):
-        values = x_cot[h].astype(f32)
-        for part in range(2):
-            store_shifts(xs2, part, h, values[part * half : (part + 1) * half])
+
+    def share(x, at):
+        return remote(x.at[k], x.at[k], d_send.at[at], d_recv.at[at], rows=sibling)
+
+    def shift_rows(x, xs):
+        for h in range(rows):
+            values = x[h % 2, h // 2].astype(f32)
+            for part in range(2):
+                store_shifts(xs, part, h, values[part * half : (part + 1) * half])
+
+    share(x_cot, 0).start()
+    lend_cot = remote(x_cot.at[k], x_far.at[k], c_send.at[1], c_recv.at[1], dp=partner)
+    lend_hid = remote(hid_b.at[lent], hid_far, h_send.at[1], h_recv.at[1], dp=partner)
+
+    @pl.when(jnp.logical_not(middle))
+    def _():
+        lend_cot.start()
+
+    forward(0, w2, 1, 2)
+    share(x_cot, 0).wait_recv()
+    shift_rows(x_cot, xs2)
 
     def conv(w, origin, xs):
         for h in range(0, rows, 2):
@@ -387,24 +402,30 @@
             total = total + y_ref[h - 1, 2 * half : 3 * half]
         return total
 
-    def conv_two(origin):
-        conv(w2, origin, xs2)
+    def conv_two(origin, xs, p, q, send, recv):
+        conv(w2, origin, xs)
         for h in range(0, rows, 2):
             low, high = row_of(h), row_of(h + 1)
             for j in range(2):
                 both = [low[j * GSIZE : (j + 1) * GSIZE], high[j * GSIZE : (j + 1) * GSIZE]]
-                p1[origin, j, h // 2] = jnp.concatenate(both, axis=0).astype(bf16)
-        slot = origin // 2
+                p[j, h // 2] = jnp.concatenate(both, axis=0).astype(bf16)
         for j in range(2):
             to = 2 * (2 * k + j) + lax.rem(origin, 2)
 
             @pl.when(to != r)
             def _():
-                remote(p1.at[origin, j], q1.at[slot, c], p_send.at[0], p_recv.at[slot], rows=to).start()
+                remote(p.at[j], q.at[c], send, recv, rows=to).start()
 
             @pl.when(to == r)
             def _():
-                q1[slot, c] = p1[origin, j]
+                q[c] = p[j]
+
+    def conv_own(origin):
+        slot = origin // 2
+        conv_two(origin, xs2, p1.at[origin], q1.at[slot], p_send.at[0], p_recv.at[slot])
+
+    def conv_far(step):
+        conv_two(nth(step), xs_far, p_far.at[step - 2], q_far, p_send.at[1], p_recv.at[2])
 
     def conv_one(origin):
         conv(w1, origin, xs1)
@@ -415,47 +436,8 @@
             remote(p2.at[origin, to], q2.at[origin, r], o_send.at[0], o_recv.at[origin], rows=to).start()
         q2[origin, r] = p2[origin, r]
 
-    forward(0, w2, 1, 2)
-    forward(0, w2, 2, 2)
-    conv_two(d)
+    conv_own(d)
     forward(0, w2, 1, 3)
-    forward(0, w2, 2, 3)
-    take(0, w2, 1)
-    conv_two(nth(1))
-
-    def activation(normed, gain, shift):
-        linear = normed * gain + shift
-        logistic = 1.0 / (1.0 + jnp.exp(-linear))
-        return logistic * (1.0 + linear * (1.0 - logistic)) * gain
-
-    everyone = hid_b.at[0 : rows - 1]
-    wait_group(everyone, everyone, h_send.at[0], h_recv.at[0])
-    plain = jnp.zeros((2 * GSIZE, lanes), f32)
-    square = jnp.zeros((2 * GSIZE, lanes), f32)
-    for h in range(rows):
-        values = hid_b[h].astype(f32)
-        plain += values
-        square += values * values
-
-    def two_means(values):
-        per_lane = jnp.sum(values.reshape(2, GSIZE, lanes), axis=1)
-        return image_totals(per_lane) * (1.0 / number)
-
-    average2 = two_means(plain)
-    inverse2 = lax.rsqrt(two_means(square) - average2 * average2 + 1e-05)
-    inv2_ref[...] = inverse2
-    for slot in range(2):
-        at = pl.multiple_of((k + 2 * slot) * block + GSIZE * c, GSIZE)
-        gain = par_ref[pl.ds(at, GSIZE), 2:3]
-        shift = par_ref[pl.ds(at, GSIZE), 3:4]
-        for h in range(rows):
-            values = hid_b[h].astype(f32)[slot * GSIZE : (slot + 1) * GSIZE]
-            normed = (values - average2[slot : slot + 1]) * inverse2[slot : slot + 1]
-            spot = (h % 2) * GSIZE
-            nrm2[slot, h // 2, spot : spot + GSIZE] = normed
-            act2[slot, h // 2, spot : spot + GSIZE] = activation(normed, gain, shift)
-
-    forward(0, w2, 3, 0)
     for count, here in ((chips - 1, own), (chips, jnp.logical_not(own))):
         @pl.when(here)
         def _():
@@ -468,25 +450,80 @@
                 at = side * half + j * GSIZE
                 w1[d, part, :, at : at + GSIZE] = r1[2 * j + part, :, side * GSIZE : (side + 1) * GSIZE]
 
-    for way, here in ((0, 2 * d < depth), (1, 2 * d >= depth)):
-        @pl.when(here)
-        def _():
-            for part in (k, 1 - k):
-                start_hops(1, w1, part, (way,))
-
-    forward(0, w2, 3, 1)
-    take(0, w2, 2)
-    conv_two(nth(2))
-    forward(0, w2, 3, 2)
-    forward(0, w2, 3, 3)
-    for way, here in ((0, 2 * d >= depth), (1, 2 * d < depth)):
-        @pl.when(here)
-        def _():
-            for part in (k, 1 - k):
-                start_hops(1, w1, part, (way,))
-
-    take(0, w2, 3)
-    conv_two(nth(3))
+    def start_inner(toward):
+        for here, way in ((1, toward), (2, 1 - toward)):
+            @pl.when(d == here)
+            def _():
+                start_hops(1, w1, k, (way,))
+                start_hops(1, w1, 1 - k, (way,))
+
+    start_inner(1)
+
+    take_end(0, w2, 1)
+    conv_own(nth(1))
+    @pl.when(middle)
+    def _():
+        take(0, w2, 2)
+        conv_own(nth(2))
+
+    def activation(normed, gain, shift):
+        linear = normed * gain + shift
+        logistic = 1.0 / (1.0 + jnp.exp(-linear))
+        return logistic * (1.0 + linear * (1.0 - logistic)) * gain
+
+    everyone = hid_two.at[0 : rows - 1]
+    wait_group(everyone, everyone, h_send.at[0], h_recv.at[0])
+
+    @pl.when(jnp.logical_not(middle))
+    def _():
+        lend_hid.start()
+        start_hops(1, w1, k)
+        start_hops(1, w1, 1 - k)
+
+    def field_stats(field, slot, nrm, act, inverse_at):
+        plain = jnp.zeros((GSIZE, lanes), f32)
+        square = jnp.zeros((GSIZE, lanes), f32)
+        for h in range(rows):
+            values = field[h].astype(f32)
+            plain += values
+            square += values * values
+        average = image_totals(jnp.sum(plain, axis=0, keepdims=True)) * (1.0 / number)
+        meansq = image_totals(jnp.sum(square, axis=0, keepdims=True)) * (1.0 / number)
+        inverse = lax.rsqrt(meansq - average * average + 1e-05)
+        inv2_ref[inverse_at : inverse_at + 1] = inverse
+        at = pl.multiple_of((k + 2 * slot) * block + GSIZE * c, GSIZE)
+        gain = par_ref[pl.ds(at, GSIZE), 2:3]
+        shift = par_ref[pl.ds(at, GSIZE), 3:4]
+        for h in range(rows):
+            normed = (field[h].astype(f32) - average) * inverse
+            spot = (h % 2) * GSIZE
+            nrm[h // 2, spot : spot + GSIZE] = normed
+            act[h // 2, spot : spot + GSIZE] = activation(normed, gain, shift)
+
+    for slot in range(2):
+        field_stats(hid_b.at[slot], slot, nrm2.at[slot], act2.at[slot], slot)
+
+    @pl.when(middle)
+    def _():
+        lend_cot.wait_recv()
+        share(x_far, 1).start()
+        start_inner(0)
+        share(x_far, 1).wait_recv()
+        shift_rows(x_far, xs_far)
+        conv_far(2)
+        take(0, w2, 3)
+        conv_far(3)
+        conv_own(nth(3))
+
+    forward(1, w1, 2, 0)
+    forward(1, w1, 1, 0)
+    @pl.when(middle)
+    def _():
+        lend_hid.wait_recv()
+        field_stats(hid_far, lent, nrm_far, act_far, 2)
+
+    forward(1, w1, 2, 1)
+    forward(1, w1, 1, 1)
 
     average1, meansq1 = wait_sums(0)
     inverse1 = lax.rsqrt(meansq1 - average1 * average1 + 1e-05)
@@ -496,37 +533,62 @@
         nrm1[rows_g, :] = normed
         act1[rows_g, :] = activation(normed, par_ref[rows_g, 0:1], par_ref[rows_g, 1:2])
 
-    for index in range(4):
-        forward(1, w1, 1, index)
-        forward(1, w1, 2, index)
-
-    for count, here in ((chips - 1, own), (chips, jnp.logical_not(own))):
-        @pl.when(here)
-        def _():
-            for slot in range(2):
-                span = q1.at[slot, 0:count]
-                wait_group(span, span, p_send.at[0], p_recv.at[slot])
-
-    hg = []
-    for slot in range(2):
+    forward(1, w1, 2, 2)
+    forward(1, w1, 1, 2)
+    def norm_two(slot, recv, q, nrm, act, inverse, dst):
+        for count, here in ((chips - 1, own), (chips, jnp.logical_not(own))):
+            @pl.when(here)
+            def _():
+                span = q.at[0:count]
+                wait_group(span, span, p_send.at[0], recv)
+
         sum_first = jnp.zeros((2 * GSIZE, lanes), f32)
         sum_second = jnp.zeros((2 * GSIZE, lanes), f32)
         scaled = []
         for m in range(rows // 2):
-            total = q1[slot, 0, m].astype(f32)
+            total = q[0, m].astype(f32)
             for frm in range(1, chips):
-                total = total + q1[slot, frm, m].astype(f32)
-            value = total * act2[slot, m]
+                total = total + q[frm, m].astype(f32)
+            value = total * act[m]
             scaled.append(value)
             sum_first += value
-            sum_second += value * nrm2[slot, m]
+            sum_second += value * nrm[m]
         first = image_totals(jnp.sum(sum_first, axis=0, keepdims=True)) * (1.0 / number)
         second = image_totals(jnp.sum(sum_second, axis=0, keepdims=True)) * (1.0 / number)
-        inverse = inv2_ref[slot : slot + 1]
-        hg.append([inverse * (scaled[m] - first - nrm2[slot, m] * second) for m in range(rows // 2)])
+        for m in range(rows // 2):
+            dst[m] = (inverse * (scaled[m] - first - nrm[m] * second)).astype(bf16)
+
+    def norm_own(slot):
+        norm_two(
+            slot, p_recv.at[slot], q1.at[slot], nrm2.at[slot], act2.at[slot],
+            inv2_ref[pl.ds(slot, 1), :], hg_two.at[slot],
+        )
+
+    lend = remote(hg_far, hg_two.at[lent], e_send.at[0], e_recv.at[0], dp=partner)
+
+    @pl.when(middle)
+    def _():
+        norm_two(lent, p_recv.at[2], q_far, nrm_far, act_far, inv2_ref[2:3, :], hg_far)
+        lend.start()
+
+    forward(1, w1, 2, 3)
+    forward(1, w1, 1, 3)
+    forward(1, w1, 3, 0)
+    forward(1, w1, 3, 1)
+    @pl.when(middle)
+    def _():
+        norm_own(0)
+        norm_own(1)
+
+    @pl.when(jnp.logical_not(middle))
+    def _():
+        norm_own(1 - lent)
+        lend.wait_recv()
+
     for h in range(rows):
         spot = (h % 2) * GSIZE
-        hg_s[h] = jnp.concatenate([hg[slot][h // 2][spot : spot + GSIZE] for slot in range(2)], axis=0).astype(bf16)
+        both = [hg_two[slot, h // 2].astype(f32)[spot : spot + GSIZE] for slot in range(2)]
+        hg_s[h] = jnp.concatenate(both, axis=0).astype(bf16)
     swap = remote(hg_s, hg_r, b_send.at[1], b_recv.at[1], rows=sibling)
     swap.start()
     pending.append(swap)
@@ -536,16 +598,14 @@
     for h in range(rows):
         store_shifts(xs1, 1 - k, h, hg_r[h].astype(f32))
 
-    forward(1, w1, 3, 0)
+    forward(1, w1, 3, 2)
     conv_one(d)
-    forward(1, w1, 3, 1)
-    take(1, w1, 1)
+    take_end(1, w1, 1)
     conv_one(nth(1))
-    forward(1, w1, 3, 2)
-    take(1, w1, 2)
+    forward(1, w1, 3, 3)
+    take_end(1, w1, 2)
     conv_one(nth(2))
-    forward(1, w1, 3, 3)
-    take(1, w1, 3)
+    take_end(1, w1, 3)
     conv_one(nth(3))
     for origin in range(depth):
         span = q2.at[origin, 0 : rows - 1]
@@ -572,8 +632,9 @@
     def sent(span, send, recv):
         remote(span, span, send, recv, rows=sibling).wait_send()
 
-    sent(x_cot.at[0 : rows - 1], c_send.at[0], c_recv.at[0])
-    sent(hid_b.at[0 : rows - 1], h_send.at[0], h_recv.at[0])
+    sent(x_cot.at[0, 0 : chips - 1], c_send.at[0], c_recv.at[0])
+    share(x_cot, 0).wait_send()
+    sent(hid_two.at[0 : rows - 1], h_send.at[0], h_recv.at[0])
     for which in range(2):
         sent(st_b.at[which, 0 : rows - 1], t_send.at[which], t_recv.at[which])
     sent(p2.at[:, 0 : rows - 1], o_send.at[0], o_recv.at[0])
@@ -581,10 +642,32 @@
         @pl.when(here)
         def _():
             sent(r1.at[0:count], f_send.at[0], f_recv.at[0])
-            sent(q1.at[:, 0:count], p_send.at[0], p_recv.at[0])
-
-    wait_hops(0, w2)
-    wait_hops(1, w1)
+
+            @pl.when(middle)
+            def _():
+                sent(q1.at[:, 0:count], p_send.at[0], p_recv.at[0])
+                sent(q_far.at[0:count], p_send.at[1], p_recv.at[2])
+
+            @pl.when(jnp.logical_not(middle))
+            def _():
+                sent(q1.at[0, 0:count], p_send.at[0], p_recv.at[0])
+
+    @pl.when(middle)
+    def _():
+        share(x_far, 1).wait_send()
+        lend.wait_send()
+
+    @pl.when(jnp.logical_not(middle))
+    def _():
+        lend_cot.wait_send()
+        lend_hid.wait_send()
+
+    last = depth - 1
+    wait_hops(0, w2, [(0, 0, 0, 1), (1, 0, 0, 2), (1, 1, 1, 2), (2, 0, 2, 3), (2, 1, 2, 4), (3, 1, 3, 4)])
+    wait_hops(
+        1, w1,
+        [(here, 0, 0, here + 1) for here in range(last)] + [(here, 1, here, depth) for here in range(1, depth)],
+    )
 
 
 def kernel_body(
@@ -618,9 +701,8 @@
             pltpu.VMEM((channels,), f32),
             dma((9,)),
             pltpu.VMEM((channels, lanes), bf16),
-            pltpu.VMEM((rows, block, lanes), bf16),
-            pltpu.VMEM((rows, 2 * GSIZE, lanes), bf16),
-            pltpu.VMEM((rows, 2 * GSIZE, lanes), bf16),
+            pltpu.VMEM((2, chips, block, lanes), bf16),
+            pltpu.VMEM((2, rows, GSIZE, lanes), bf16),
             pltpu.VMEM((depth, 2, 3 * half, wide), bf16),
             pltpu.VMEM((depth, 2, 3 * half, wide), bf16),
             pltpu.VMEM((2, 2, 3 * half, narrow), bf16),
@@ -639,26 +721,43 @@
             pltpu.VMEM((channels, lanes), f32),
             pltpu.VMEM((2, rows // 2, 2 * GSIZE, lanes), f32),
             pltpu.VMEM((2, rows // 2, 2 * GSIZE, lanes), f32),
-            pltpu.VMEM((2, lanes), f32),
+            pltpu.VMEM((4, lanes), f32),
             pltpu.VMEM((2, groups // 2, lanes), f32),
             pltpu.VMEM((2, rows, groups // 2, lanes), f32),
             pltpu.VMEM((channels, 8), f32),
+            pltpu.VMEM((2, chips, block, lanes), bf16),
+            pltpu.VMEM((rows, 2, GSIZE, lanes), bf16),
+            pltpu.VMEM((rows, GSIZE, lanes), bf16),
+            pltpu.VMEM((2, rows, wide, lanes), bf16),
+            pltpu.VMEM((2, 2, rows // 2, 2 * GSIZE, lanes), bf16),
+            pltpu.VMEM((chips, rows // 2, 2 * GSIZE, lanes), bf16),
+            pltpu.VMEM((rows // 2, 2 * GSIZE, lanes), f32),
+            pltpu.VMEM((rows // 2, 2 * GSIZE, lanes), f32),
+            pltpu.VMEM((rows // 2, 2 * GSIZE, lanes), bf16),
+            pltpu.VMEM((2, rows // 2, 2 * GSIZE, lanes), bf16),
             dma((2, 2)), dma((2, depth, 2, 2)),
             dma((1,)), dma((1,)),
             dma((2,)), dma((2,)),
-            dma((1,)), dma((1,)),
-            dma((1,)), dma((1,)),
-            dma((1,)), dma((2,)),
+            dma((2,)), dma((2,)),
+            dma((2,)), dma((2,)),
+            dma((2,)), dma((3,)),
             dma((1,)), dma((depth,)),
             dma((2,)), dma((2,)),
+            dma((2,)), dma((2,)),
+            dma((1,)), dma((1,)),
         ],
         compiler_params=pltpu.CompilerParams(
-            collective_id=0, has_side_effects=True
+            collective_id=0, has_side_effects=True, vmem_limit_bytes=48 * 1024 * 1024
         ),
     )(
-        latent.reshape(lanes, channels), hidden.reshape(lanes, channels),
-        cotangent.reshape(lanes, channels), filter_one, filter_two,
-        gain_one, shift_one, gain_two, shift_two,
+        *[
+            pltpu.with_memory_space_constraint(array, pltpu.HBM)
+            for array in (
+                latent.reshape(lanes, channels), hidden.reshape(lanes, channels),
+                cotangent.reshape(lanes, channels), filter_one, filter_two,
+                gain_one, shift_one, gain_two, shift_two,
+            )
+        ]
     )
     return out.reshape(latent.shape)
 

time: 48.7 us -> 44.7 us (0.918)
  Pallas kernels: 47 us -> 43.9 us
  local copies, waits for them, and re-layouts: 1.6 us -> 0.67 us
    pallas_call x1, Pallas kernels: 47 us -> 43.9 us  [kernel_body(): pl.pallas_call(functools.partial(kernel, depth, rows, breadth), out_shape...]
    unnamed x1, local copies, waits for them, and re-layouts: 1.6 us -> 0.67 us
where the time goes in v3:
time: 44.7 us; the launch traced here: 44.6 us
  Pallas kernels  43.9 us (98%)
  local copies, waits for them, and re-layouts  0.67 us (1%)
    pallas_call x1, Pallas kernels, kernel_body(): pl.pallas_call(functools.partial(kernel, depth, rows, breadth), out_shape...  43.9 us

profile of v3, /device:TPU:0, one launch (start us, length us, event | category | flops | bytes accessed | tf_op | source)
XLA Modules:
  0.0 44.6 jit_solution(5300101577233558276)
XLA Ops:
  0.0 43.9 %shard_map.91 = bf16[128,640]{1,0:T(8,128)(2,1)S(1)} custom-call(bf16[128,640]{1,0:T(8,128)(2,1)} %bitcast.7, bf16[128,640]{1,0:T(8,128)(2,1)} %bitcast.8, bf16[128,640]{1,0:T(8,128)(2,1)} %bitcast.9, bf16[9,160,80]{2,1,0:T(8,128)(2,1)} %raw1_hbm.1, bf16[9,160,80]{2,1,0:T(8,128)(2,1)} %raw2_hbm.1, f32[640]{0:T(1024)} %gain1_hbm.1, f32[640]{0:T(1024)} %shift1_hbm.1, ...), custom_call_target="tpu_custom_call" | custom-call | tf_op jit(solution)/shard_map/pallas_call | solution.py:687
  43.9 0.7 %copy.12 = bf16[2,1,64,640]{3,2,1,0:T(8,128)(2,1)} copy(bf16[2,1,64,640]{3,2,1,0:T(8,128)(2,1)S(1)} %bitcast.6) | data formatting | bytes 327680

commit v4 on v3

--- a/solution.py
+++ b/solution.py
@@ -120,7 +120,7 @@
     block = channels // depth
     half = block // 2
     images = lanes // breadth
-    wide = w1.shape[3]
+    wide = w1.shape[4]
     number = rows * breadth * GSIZE
     groups = channels // GSIZE
     bf16, f32 = jnp.bfloat16, jnp.float32
@@ -130,22 +130,6 @@
             src_ref=src, dst_ref=dst, send_sem=send, recv_sem=recv,
             device_id=device, device_id_type=MESH,
         )
-
-    barrier = pltpu.get_barrier_semaphore()
-
-    middle = (d > 0) & (d < depth - 1)
-    partner = d + 1 - 2 * lax.rem(d, 2)
-    lent = jnp.where(2 * d < depth, 1, 0)
-
-    @pl.when(middle)
-    def _():
-        pl.semaphore_signal(barrier, inc=1, device_id={"dp": depth - 1 - d}, device_id_type=MESH)
-
-    for to in range(rows):
-        pl.semaphore_signal(barrier, inc=1, device_id={"dp": partner, "rows": to}, device_id_type=MESH)
-
-    for off in range(1, rows):
-        pl.semaphore_signal(barrier, inc=1, device_id={"rows": lax.rem(r + off, rows)}, device_id_type=MESH)
 
     pending = []
     loads = {
@@ -156,17 +140,37 @@
             ("shift1", shift1_hbm, shift1), ("gain2", gain2_hbm, gain2), ("shift2", shift2_hbm, shift2),
         ))
     }
-    for load in loads.values():
-        load.start()
+    loads["raw2"].start()
+
+    barrier = pltpu.get_barrier_semaphore()
+
+    middle = (d > 0) & (d < depth - 1)
+    partner = d + 1 - 2 * lax.rem(d, 2)
+    lent = jnp.where(2 * d < depth, 1, 0)
+
+    @pl.when(d > 0)
+    def _():
+        pl.semaphore_signal(barrier, inc=1, device_id={"dp": d - 1}, device_id_type=MESH)
+
+    @pl.when(d < depth - 1)
+    def _():
+        pl.semaphore_signal(barrier, inc=1, device_id={"dp": d + 1}, device_id_type=MESH)
+
+    for off in range(1, rows):
+        pl.semaphore_signal(barrier, inc=1, device_id={"rows": lax.rem(r + off, rows)}, device_id_type=MESH)
+
+    for name, load in loads.items():
+        if name != "raw2":
+            load.start()
 
     pad = wide - 3 * half
     own = k == c // 2
-    w2[d, k, :, 3 * half :] = jnp.zeros((3 * half, pad), bf16)
-    s2[:, 3 * half :] = jnp.zeros((3 * half, pad), bf16)
+    w2[d, k, :, :, 3 * half :] = jnp.zeros((3, half, pad), bf16)
+    s2[:, :, 3 * half :] = jnp.zeros((3, half, pad), bf16)
     for part in range(2):
-        w1[d, part, :, 3 * half :] = jnp.zeros((3 * half, pad), bf16)
+        w1[d, part, :, :, 3 * half :] = jnp.zeros((3, half, pad), bf16)
         for side_core in range(2):
-            s1[part, side_core, :, 3 * GSIZE :] = jnp.zeros((3 * half, s1.shape[3] - 3 * GSIZE), bf16)
+            s1[part, side_core, :, :, 3 * GSIZE :] = jnp.zeros((3, half, s1.shape[4] - 3 * GSIZE), bf16)
     for xs in (xs1, xs2, xs_far):
         for part in range(2):
             for h in range(rows):
@@ -177,20 +181,20 @@
         start = pl.multiple_of(which * half, 16)
         for tap in range(TAPS):
             down, side = tap // 3, tap % 3
-            ready[down * half : (down + 1) * half, side * half : (side + 1) * half] = raw[
+            ready[down, :, side * half : (side + 1) * half] = raw[
                 tap, pl.ds(start, half), :
             ]
 
     arrange(w2.at[d, k], raw2, k)
-    arrange(s2, raw2, 1 - k)
-
-    pl.semaphore_wait(barrier, 2 * rows - 1 + jnp.where(middle, 1, 0))
-
-    segments = ((0, 128), (128, 3 * half))
+
+    pl.semaphore_wait(barrier, rows + jnp.where(middle, 1, 0))
+
+    split = half // 32 * 16 + 16
+    segments = ((0, split), (split, half))
 
     def hop(which, w, origin, part, seg, way):
         low, high = segments[seg]
-        piece = w.at[origin, part, low:high]
+        piece = w.at[origin, part, :, low:high]
         return remote(
             piece, piece, z_send.at[which, way], z_recv.at[which, origin, part, seg], dp=d + 1 - 2 * way
         )
@@ -201,16 +205,22 @@
         value = step - near if step == 1 else step
         return jnp.where(2 * d < depth, value, depth - 1 - value)
 
-    def start_hops(which, w, part, ways=(0, 1)):
+    def start_hops(which, w, part, ways=(0, 1), segs=(0, 1)):
         for way in ways:
             @pl.when((d < depth - 1) if way == 0 else (d > 0))
             def _():
-                for seg in range(2):
+                for seg in segs:
                     hop(which, w, d, part, seg, way).start()
+
+    def start_one(ways):
+        for seg in range(2):
+            for part in (k, 1 - k):
+                start_hops(1, w1, part, ways, (seg,))
 
     def forward(which, w, step, index):
         origin = nth(step)
-        part, seg = (k, 1 - k)[index // 2], index % 2
+        at, seg = (index // 2, index % 2) if which == 0 else (index % 2, index // 2)
+        part = (k, 1 - k)[at]
         for way in range(2):
             @pl.when(middle & ((origin < d) if way == 0 else (origin > d)))
             def _():
@@ -218,15 +228,15 @@
                 copy.wait_recv()
                 copy.start()
 
-    def take(which, w, step):
+    def take(which, w, step, segs=(0, 1)):
         for part in (k, 1 - k):
-            for seg in range(2):
+            for seg in segs:
                 hop(which, w, nth(step), part, seg, 0).wait_recv()
 
-    def take_end(which, w, step):
+    def take_end(which, w, step, segs=(0, 1)):
         @pl.when(jnp.logical_not(middle))
         def _():
-            take(which, w, step)
+            take(which, w, step, segs)
 
     def wait_hops(which, w, spans):
         for here, way, low, high in spans:
@@ -238,6 +248,7 @@
                 ).wait_send()
 
     start_hops(0, w2, k)
+    arrange(s2, raw2, 1 - k)
     twin = remote(s2, w2.at[d, k], b_send.at[0], b_recv.at[0], rows=sibling)
     twin.start()
     pending.append(twin)
@@ -259,7 +270,7 @@
             ready = s1.at[part, side_core]
             for tap in range(TAPS):
                 down, side = tap // 3, tap % 3
-                ready[down * half : (down + 1) * half, side * GSIZE : (side + 1) * GSIZE] = raw1[
+                ready[down, :, side * GSIZE : (side + 1) * GSIZE] = raw1[
                     tap, side_core * half : (side_core + 1) * half, part * GSIZE : (part + 1) * GSIZE
                 ]
 
@@ -384,28 +395,29 @@
     share(x_cot, 0).wait_recv()
     shift_rows(x_cot, xs2)
 
-    def conv(w, origin, xs):
+    def conv(w, origin, xs, low, high):
         for h in range(0, rows, 2):
             total = None
             for part in range(2):
                 pair = jnp.concatenate([xs[part, h], xs[part, h + 1]], axis=1)
-                term = jnp.dot(w[origin, part], pair, preferred_element_type=f32)
+                piece = w[origin, part, :, low:high].reshape(3 * (high - low), wide)
+                term = jnp.dot(piece, pair, preferred_element_type=f32)
                 total = term if total is None else total + term
-            y_ref[h] = total[:, :lanes]
-            y_ref[h + 1] = total[:, lanes:]
-
-    def row_of(h):
-        total = y_ref[h, half : 2 * half]
+            y_ref[h, 0 : 3 * (high - low)] = total[:, :lanes]
+            y_ref[h + 1, 0 : 3 * (high - low)] = total[:, lanes:]
+
+    def row_of(h, size):
+        total = y_ref[h, size : 2 * size]
         if h + 1 < rows:
-            total = total + y_ref[h + 1, 0:half]
+            total = total + y_ref[h + 1, 0:size]
         if h > 0:
-            total = total + y_ref[h - 1, 2 * half : 3 * half]
+            total = total + y_ref[h - 1, 2 * size : 3 * size]
         return total
 
     def conv_two(origin, xs, p, q, send, recv):
-        conv(w2, origin, xs)
+        conv(w2, origin, xs, 0, half)
         for h in range(0, rows, 2):
-            low, high = row_of(h), row_of(h + 1)
+            low, high = row_of(h, half), row_of(h + 1, half)
             for j in range(2):
                 both = [low[j * GSIZE : (j + 1) * GSIZE], high[j * GSIZE : (j + 1) * GSIZE]]
                 p[j, h // 2] = jnp.concatenate(both, axis=0).astype(bf16)
@@ -427,14 +439,16 @@
     def conv_far(step):
         conv_two(nth(step), xs_far, p_far.at[step - 2], q_far, p_send.at[1], p_recv.at[2])
 
-    def conv_one(origin):
-        conv(w1, origin, xs1)
+    def conv_one(origin, low=0, high=half):
+        conv(w1, origin, xs1, low, high)
         for h in range(rows):
-            p2[origin, h] = row_of(h).astype(bf16)
+            p2[origin, h, low:high] = row_of(h, high - low).astype(bf16)
         for off in range(1, rows):
             to = lax.rem(r + off, rows)
-            remote(p2.at[origin, to], q2.at[origin, r], o_send.at[0], o_recv.at[origin], rows=to).start()
-        q2[origin, r] = p2[origin, r]
+            remote(
+                p2.at[origin, to, low:high], q2.at[origin, r, low:high], o_send.at[0], o_recv.at[origin], rows=to
+            ).start()
+        q2[origin, r, low:high] = p2[origin, r, low:high]
 
     conv_own(d)
     forward(0, w2, 1, 3)
@@ -448,14 +462,13 @@
         for j in range(2):
             for side in range(3):
                 at = side * half + j * GSIZE
-                w1[d, part, :, at : at + GSIZE] = r1[2 * j + part, :, side * GSIZE : (side + 1) * GSIZE]
+                w1[d, part, :, :, at : at + GSIZE] = r1[2 * j + part, :, :, side * GSIZE : (side + 1) * GSIZE]
 
     def start_inner(toward):
         for here, way in ((1, toward), (2, 1 - toward)):
             @pl.when(d == here)
             def _():
-                start_hops(1, w1, k, (way,))
-                start_hops(1, w1, 1 - k, (way,))
+                start_one((way,))
 
     start_inner(1)
 
@@ -477,8 +490,7 @@
     @pl.when(jnp.logical_not(middle))
     def _():
         lend_hid.start()
-        start_hops(1, w1, k)
-        start_hops(1, w1, 1 - k)
+        start_one((0, 1))
 
     def field_stats(field, slot, nrm, act, inverse_at):
         plain = jnp.zeros((GSIZE, lanes), f32)
@@ -533,8 +545,6 @@
         nrm1[rows_g, :] = normed
         act1[rows_g, :] = activation(normed, par_ref[rows_g, 0:1], par_ref[rows_g, 1:2])
 
-    forward(1, w1, 2, 2)
-    forward(1, w1, 1, 2)
     def norm_two(slot, recv, q, nrm, act, inverse, dst):
         for count, here in ((chips - 1, own), (chips, jnp.logical_not(own))):
             @pl.when(here)
@@ -571,6 +581,8 @@
         norm_two(lent, p_recv.at[2], q_far, nrm_far, act_far, inv2_ref[2:3, :], hg_far)
         lend.start()
 
+    forward(1, w1, 2, 2)
+    forward(1, w1, 1, 2)
     forward(1, w1, 2, 3)
     forward(1, w1, 1, 3)
     forward(1, w1, 3, 0)
@@ -703,11 +715,11 @@
             pltpu.VMEM((channels, lanes), bf16),
             pltpu.VMEM((2, chips, block, lanes), bf16),
             pltpu.VMEM((2, rows, GSIZE, lanes), bf16),
-            pltpu.VMEM((depth, 2, 3 * half, wide), bf16),
-            pltpu.VMEM((depth, 2, 3 * half, wide), bf16),
-            pltpu.VMEM((2, 2, 3 * half, narrow), bf16),
-            pltpu.VMEM((3 * half, wide), bf16),
-            pltpu.VMEM((chips, 3 * half, narrow), bf16),
+            pltpu.VMEM((depth, 2, 3, half, wide), bf16),
+            pltpu.VMEM((depth, 2, 3, half, wide), bf16),
+            pltpu.VMEM((2, 2, 3, half, narrow), bf16),
+            pltpu.VMEM((3, half, wide), bf16),
+            pltpu.VMEM((chips, 3, half, narrow), bf16),
             pltpu.VMEM((2, rows, wide, lanes), bf16),
             pltpu.VMEM((2, rows, wide, lanes), bf16),
             pltpu.VMEM((rows, 3 * half, lanes), f32),

time: 44.7 us -> 43.9 us (0.982)
  Pallas kernels: 43.9 us -> 43.1 us
    pallas_call x1, Pallas kernels: 43.9 us -> 43.1 us  [kernel_body(): pl.pallas_call(functools.partial(kernel, depth, rows, breadth), out_shape...]
where the time goes in v4:
time: 43.9 us; the launch traced here: 43.7 us
  Pallas kernels  43.1 us (98%)
  local copies, waits for them, and re-layouts  0.67 us (2%)
    pallas_call x1, Pallas kernels, kernel_body(): pl.pallas_call(functools.partial(kernel, depth, rows, breadth), out_shape...  43.1 us

profile of v4, /device:TPU:0, one launch (start us, length us, event | category | flops | bytes accessed | tf_op | source)
XLA Modules:
  0.0 43.7 jit_solution(8691985404717844265)
XLA Ops:
  0.0 43.1 %shard_map.91 = bf16[128,640]{1,0:T(8,128)(2,1)S(1)} custom-call(bf16[128,640]{1,0:T(8,128)(2,1)} %bitcast.7, bf16[128,640]{1,0:T(8,128)(2,1)} %bitcast.8, bf16[128,640]{1,0:T(8,128)(2,1)} %bitcast.9, bf16[9,160,80]{2,1,0:T(8,128)(2,1)} %raw1_hbm.1, bf16[9,160,80]{2,1,0:T(8,128)(2,1)} %raw2_hbm.1, f32[640]{0:T(1024)} %gain1_hbm.1, f32[640]{0:T(1024)} %shift1_hbm.1, ...), custom_call_target="tpu_custom_call" | custom-call | tf_op jit(solution)/shard_map/pallas_call | solution.py:699
  43.1 0.7 %copy.12 = bf16[2,1,64,640]{3,2,1,0:T(8,128)(2,1)} copy(bf16[2,1,64,640]{3,2,1,0:T(8,128)(2,1)S(1)} %bitcast.6) | data formatting | bytes 327680

commit v5 on v4

--- a/solution.py
+++ b/solution.py
@@ -120,7 +120,7 @@
     block = channels // depth
     half = block // 2
     images = lanes // breadth
-    wide = w1.shape[4]
+    wide = w1.shape[3]
     number = rows * breadth * GSIZE
     groups = channels // GSIZE
     bf16, f32 = jnp.bfloat16, jnp.float32
@@ -165,10 +165,11 @@
 
     pad = wide - 3 * half
     own = k == c // 2
-    w2[d, k, :, :, 3 * half :] = jnp.zeros((3, half, pad), bf16)
-    s2[:, :, 3 * half :] = jnp.zeros((3, half, pad), bf16)
+    tall = 3 * half
+    w2[d, k, :, tall:] = jnp.zeros((tall, pad), bf16)
+    s2[:, tall:] = jnp.zeros((tall, pad), bf16)
     for part in range(2):
-        w1[d, part, :, :, 3 * half :] = jnp.zeros((3, half, pad), bf16)
+        w1[d, part, :, tall:] = jnp.zeros((tall, pad), bf16)
         for side_core in range(2):
             s1[part, side_core, :, :, 3 * GSIZE :] = jnp.zeros((3, half, s1.shape[4] - 3 * GSIZE), bf16)
     for xs in (xs1, xs2, xs_far):
@@ -181,22 +182,31 @@
         start = pl.multiple_of(which * half, 16)
         for tap in range(TAPS):
             down, side = tap // 3, tap % 3
-            ready[down, :, side * half : (side + 1) * half] = raw[
+            ready[down * half : (down + 1) * half, side * half : (side + 1) * half] = raw[
                 tap, pl.ds(start, half), :
             ]
 
+    def pack(ready):
+        for at in range((tall - 128) // pad):
+            ready[pad * at : pad * (at + 1), tall:] = ready[tall - pad :, 128 + pad * at : 128 + pad * (at + 1)]
+
+    def unpack(w, origin):
+        for part in range(2):
+            pieces = [w[origin, part, pad * at : pad * (at + 1), tall:] for at in range((tall - 128) // pad)]
+            full = jnp.concatenate(pieces + [jnp.zeros((pad, pad), bf16)], axis=1)
+            w[origin, part, tall - pad :, 128:] = full
+
     arrange(w2.at[d, k], raw2, k)
 
     pl.semaphore_wait(barrier, rows + jnp.where(middle, 1, 0))
 
-    split = half // 32 * 16 + 16
-    segments = ((0, split), (split, half))
+    segments = ((tall, 0, 128), (tall - pad, 128, wide))
 
     def hop(which, w, origin, part, seg, way):
-        low, high = segments[seg]
-        piece = w.at[origin, part, :, low:high]
+        deep, low, high = segments[seg]
+        piece = w.at[origin, part, 0:deep, low:high]
         return remote(
-            piece, piece, z_send.at[which, way], z_recv.at[which, origin, part, seg], dp=d + 1 - 2 * way
+            piece, piece, z_send.at[which, way, seg], z_recv.at[which, origin, part, seg], dp=d + 1 - 2 * way
         )
 
     near = jnp.minimum(d, depth - 1 - d)
@@ -213,14 +223,12 @@
                     hop(which, w, d, part, seg, way).start()
 
     def start_one(ways):
-        for seg in range(2):
-            for part in (k, 1 - k):
-                start_hops(1, w1, part, ways, (seg,))
+        for part in (k, 1 - k):
+            start_hops(1, w1, part, ways)
 
     def forward(which, w, step, index):
         origin = nth(step)
-        at, seg = (index // 2, index % 2) if which == 0 else (index % 2, index // 2)
-        part = (k, 1 - k)[at]
+        part, seg = (k, 1 - k)[index // 2], index % 2
         for way in range(2):
             @pl.when(middle & ((origin < d) if way == 0 else (origin > d)))
             def _():
@@ -242,13 +250,17 @@
         for here, way, low, high in spans:
             @pl.when(d == here)
             def _():
-                span = w.at[low:high]
-                remote(
-                    span, span, z_send.at[which, way], z_recv.at[which, 0, 0, 0], dp=d + 1 - 2 * way
-                ).wait_send()
-
-    start_hops(0, w2, k)
+                for seg, (deep, left, right) in enumerate(segments):
+                    span = w.at[low:high, :, 0:deep, left:right]
+                    remote(
+                        span, span, z_send.at[which, way, seg], z_recv.at[which, 0, 0, 0], dp=d + 1 - 2 * way
+                    ).wait_send()
+
+    start_hops(0, w2, k, segs=(0,))
+    pack(w2.at[d, k])
+    start_hops(0, w2, k, segs=(1,))
     arrange(s2, raw2, 1 - k)
+    pack(s2)
     twin = remote(s2, w2.at[d, k], b_send.at[0], b_recv.at[0], rows=sibling)
     twin.start()
     pending.append(twin)
@@ -395,29 +407,28 @@
     share(x_cot, 0).wait_recv()
     shift_rows(x_cot, xs2)
 
-    def conv(w, origin, xs, low, high):
+    def conv(w, origin, xs):
         for h in range(0, rows, 2):
             total = None
             for part in range(2):
                 pair = jnp.concatenate([xs[part, h], xs[part, h + 1]], axis=1)
-                piece = w[origin, part, :, low:high].reshape(3 * (high - low), wide)
-                term = jnp.dot(piece, pair, preferred_element_type=f32)
+                term = jnp.dot(w[origin, part], pair, preferred_element_type=f32)
                 total = term if total is None else total + term
-            y_ref[h, 0 : 3 * (high - low)] = total[:, :lanes]
-            y_ref[h + 1, 0 : 3 * (high - low)] = total[:, lanes:]
-
-    def row_of(h, size):
-        total = y_ref[h, size : 2 * size]
+            y_ref[h] = total[:, :lanes]
+            y_ref[h + 1] = total[:, lanes:]
+
+    def row_of(h):
+        total = y_ref[h, half : 2 * half]
         if h + 1 < rows:
-            total = total + y_ref[h + 1, 0:size]
+            total = total + y_ref[h + 1, 0:half]
         if h > 0:
-            total = total + y_ref[h - 1, 2 * size : 3 * size]
+            total = total + y_ref[h - 1, 2 * half : 3 * half]
         return total
 
     def conv_two(origin, xs, p, q, send, recv):
-        conv(w2, origin, xs, 0, half)
+        conv(w2, origin, xs)
         for h in range(0, rows, 2):
-            low, high = row_of(h, half), row_of(h + 1, half)
+            low, high = row_of(h), row_of(h + 1)
             for j in range(2):
                 both = [low[j * GSIZE : (j + 1) * GSIZE], high[j * GSIZE : (j + 1) * GSIZE]]
                 p[j, h // 2] = jnp.concatenate(both, axis=0).astype(bf16)
@@ -439,16 +450,14 @@
     def conv_far(step):
         conv_two(nth(step), xs_far, p_far.at[step - 2], q_far, p_send.at[1], p_recv.at[2])
 
-    def conv_one(origin, low=0, high=half):
-        conv(w1, origin, xs1, low, high)
+    def conv_one(origin):
+        conv(w1, origin, xs1)
         for h in range(rows):
-            p2[origin, h, low:high] = row_of(h, high - low).astype(bf16)
+            p2[origin, h] = row_of(h).astype(bf16)
         for off in range(1, rows):
             to = lax.rem(r + off, rows)
-            remote(
-                p2.at[origin, to, low:high], q2.at[origin, r, low:high], o_send.at[0], o_recv.at[origin], rows=to
-            ).start()
-        q2[origin, r, low:high] = p2[origin, r, low:high]
+            remote(p2.at[origin, to], q2.at[origin, r], o_send.at[0], o_recv.at[origin], rows=to).start()
+        q2[origin, r] = p2[origin, r]
 
     conv_own(d)
     forward(0, w2, 1, 3)
@@ -462,7 +471,9 @@
         for j in range(2):
             for side in range(3):
                 at = side * half + j * GSIZE
-                w1[d, part, :, :, at : at + GSIZE] = r1[2 * j + part, :, :, side * GSIZE : (side + 1) * GSIZE]
+                piece = r1[2 * j + part, :, :, side * GSIZE : (side + 1) * GSIZE]
+                w1[d, part, :, at : at + GSIZE] = piece.reshape(tall, GSIZE)
+        pack(w1.at[d, part])
 
     def start_inner(toward):
         for here, way in ((1, toward), (2, 1 - toward)):
@@ -473,10 +484,12 @@
     start_inner(1)
 
     take_end(0, w2, 1)
+    unpack(w2, nth(1))
     conv_own(nth(1))
     @pl.when(middle)
     def _():
         take(0, w2, 2)
+        unpack(w2, nth(2))
         conv_own(nth(2))
 
     def activation(normed, gain, shift):
@@ -517,13 +530,14 @@
 
     @pl.when(middle)
     def _():
+        start_inner(0)
         lend_cot.wait_recv()
         share(x_far, 1).start()
-        start_inner(0)
         share(x_far, 1).wait_recv()
         shift_rows(x_far, xs_far)
         conv_far(2)
         take(0, w2, 3)
+        unpack(w2, nth(3))
         conv_far(3)
         conv_own(nth(3))
 
@@ -613,11 +627,14 @@
     forward(1, w1, 3, 2)
     conv_one(d)
     take_end(1, w1, 1)
+    unpack(w1, nth(1))
     conv_one(nth(1))
     forward(1, w1, 3, 3)
     take_end(1, w1, 2)
+    unpack(w1, nth(2))
     conv_one(nth(2))
     take_end(1, w1, 3)
+    unpack(w1, nth(3))
     conv_one(nth(3))
     for origin in range(depth):
         span = q2.at[origin, 0 : rows - 1]
@@ -715,10 +732,10 @@
             pltpu.VMEM((channels, lanes), bf16),
             pltpu.VMEM((2, chips, block, lanes), bf16),
             pltpu.VMEM((2, rows, GSIZE, lanes), bf16),
-            pltpu.VMEM((depth, 2, 3, half, wide), bf16),
-            pltpu.VMEM((depth, 2, 3, half, wide), bf16),
+            pltpu.VMEM((depth, 2, 3 * half, wide), bf16),
+            pltpu.VMEM((depth, 2, 3 * half, wide), bf16),
             pltpu.VMEM((2, 2, 3, half, narrow), bf16),
-            pltpu.VMEM((3, half, wide), bf16),
+            pltpu.VMEM((3 * half, wide), bf16),
             pltpu.VMEM((chips, 3, half, narrow), bf16),
             pltpu.VMEM((2, rows, wide, lanes), bf16),
             pltpu.VMEM((2, rows, wide, lanes), bf16),
@@ -747,7 +764,7 @@
             pltpu.VMEM((rows // 2, 2 * GSIZE, lanes), f32),
             pltpu.VMEM((rows // 2, 2 * GSIZE, lanes), bf16),
             pltpu.VMEM((2, rows // 2, 2 * GSIZE, lanes), bf16),
-            dma((2, 2)), dma((2, depth, 2, 2)),
+            dma((2, 2, 2)), dma((2, depth, 2, 2)),
             dma((1,)), dma((1,)),
             dma((2,)), dma((2,)),
             dma((2,)), dma((2,)),

time: 43.9 us -> 42.2 us (0.961)
  Pallas kernels: 43.1 us -> 41.4 us
    pallas_call x1, Pallas kernels: 43.1 us -> 41.4 us  [kernel_body(): pl.pallas_call(functools.partial(kernel, depth, rows, breadth), out_shape...]
where the time goes in v5:
time: 42.2 us; the launch traced here: 42.1 us
  Pallas kernels  41.4 us (98%)
  local copies, waits for them, and re-layouts  0.67 us (2%)
    pallas_call x1, Pallas kernels, kernel_body(): pl.pallas_call(functools.partial(kernel, depth, rows, breadth), out_shape...  41.4 us

profile of v5, /device:TPU:0, one launch (start us, length us, event | category | flops | bytes accessed | tf_op | source)
XLA Modules:
  0.0 42.1 jit_solution(8538460332291944830)
XLA Ops:
  0.0 41.4 %shard_map.91 = bf16[128,640]{1,0:T(8,128)(2,1)S(1)} custom-call(bf16[128,640]{1,0:T(8,128)(2,1)} %bitcast.7, bf16[128,640]{1,0:T(8,128)(2,1)} %bitcast.8, bf16[128,640]{1,0:T(8,128)(2,1)} %bitcast.9, bf16[9,160,80]{2,1,0:T(8,128)(2,1)} %raw1_hbm.1, bf16[9,160,80]{2,1,0:T(8,128)(2,1)} %raw2_hbm.1, f32[640]{0:T(1024)} %gain1_hbm.1, f32[640]{0:T(1024)} %shift1_hbm.1, ...), custom_call_target="tpu_custom_call" | custom-call | tf_op jit(solution)/shard_map/pallas_call | solution.py:716
  41.4 0.7 %copy.12 = bf16[2,1,64,640]{3,2,1,0:T(8,128)(2,1)} copy(bf16[2,1,64,640]{3,2,1,0:T(8,128)(2,1)S(1)} %bitcast.6) | data formatting | bytes 327680

commit v6 on v5

--- a/solution.py
+++ b/solution.py
@@ -106,7 +106,7 @@
     cot_t, x_cot, hid_b, w1, w2, s1, s2, r1,
     xs1, xs2, y_ref, p1, q1, p2, q2, hg_s, hg_r,
     nrm1, act1, nrm2, act2, inv2_ref, st_s, st_b, par_ref,
-    x_far, hid_two, hid_far, xs_far, p_far, q_far, nrm_far, act_far, hg_far, hg_two,
+    sums_ref, x_far, hid_two, hid_far, xs_far, p_far, q_far, nrm_far, act_far, hg_far, hg_two,
     z_send, z_recv, f_send, f_recv, b_send, b_recv, c_send, c_recv, h_send, h_recv,
     p_send, p_recv, o_send, o_recv, t_send, t_recv, d_send, d_recv, e_send, e_recv,
 ):
@@ -206,7 +206,7 @@
         deep, low, high = segments[seg]
         piece = w.at[origin, part, 0:deep, low:high]
         return remote(
-            piece, piece, z_send.at[which, way, seg], z_recv.at[which, origin, part, seg], dp=d + 1 - 2 * way
+            piece, piece, z_send.at[which, way, seg], z_recv.at[which, origin - way, part, seg], dp=d + 1 - 2 * way
         )
 
     near = jnp.minimum(d, depth - 1 - d)
@@ -239,7 +239,8 @@
     def take(which, w, step, segs=(0, 1)):
         for part in (k, 1 - k):
             for seg in segs:
-                hop(which, w, nth(step), part, seg, 0).wait_recv()
+                origin = nth(step)
+                hop(which, w, origin, part, seg, jnp.where(origin > d, 1, 0)).wait_recv()
 
     def take_end(which, w, step, segs=(0, 1)):
         @pl.when(jnp.logical_not(middle))
@@ -341,12 +342,12 @@
         st_s[which] = packed
         for off in range(1, rows):
             to = lax.rem(r + off, rows)
-            remote(st_s.at[which], st_b.at[which, r], t_send.at[which], t_recv.at[which], rows=to).start()
+            remote(st_s.at[which], st_b.at[which, r], t_send.at[0], t_recv.at[which], rows=to).start()
         st_b[which, r] = packed
 
     def wait_sums(which):
         span = st_b.at[which, 0 : rows - 1]
-        remote(span, span, t_send.at[which], t_recv.at[which], rows=sibling).wait_recv()
+        remote(span, span, t_send.at[0], t_recv.at[which], rows=sibling).wait_recv()
         total = st_b[which, 0]
         for h in range(1, rows):
             total = total + st_b[which, h]
@@ -450,13 +451,13 @@
     def conv_far(step):
         conv_two(nth(step), xs_far, p_far.at[step - 2], q_far, p_send.at[1], p_recv.at[2])
 
-    def conv_one(origin):
+    def conv_one(origin, last=0):
         conv(w1, origin, xs1)
         for h in range(rows):
             p2[origin, h] = row_of(h).astype(bf16)
         for off in range(1, rows):
             to = lax.rem(r + off, rows)
-            remote(p2.at[origin, to], q2.at[origin, r], o_send.at[0], o_recv.at[origin], rows=to).start()
+            remote(p2.at[origin, to], q2.at[origin, r], o_send.at[0], o_recv.at[last], rows=to).start()
         q2[origin, r] = p2[origin, r]
 
     conv_own(d)
@@ -599,8 +600,6 @@
     forward(1, w1, 1, 2)
     forward(1, w1, 2, 3)
     forward(1, w1, 1, 3)
-    forward(1, w1, 3, 0)
-    forward(1, w1, 3, 1)
     @pl.when(middle)
     def _():
         norm_own(0)
@@ -620,12 +619,14 @@
     pending.append(swap)
     for h in range(rows):
         store_shifts(xs1, k, h, hg_s[h].astype(f32))
+    forward(1, w1, 3, 0)
     swap.wait_recv()
     for h in range(rows):
         store_shifts(xs1, 1 - k, h, hg_r[h].astype(f32))
 
+    forward(1, w1, 3, 1)
+    conv_one(d)
     forward(1, w1, 3, 2)
-    conv_one(d)
     take_end(1, w1, 1)
     unpack(w1, nth(1))
     conv_one(nth(1))
@@ -635,23 +636,30 @@
     conv_one(nth(2))
     take_end(1, w1, 3)
     unpack(w1, nth(3))
-    conv_one(nth(3))
-    for origin in range(depth):
-        span = q2.at[origin, 0 : rows - 1]
-        wait_group(span, span, o_send.at[0], o_recv.at[origin])
-
-    one, two = [], []
-    for origin in range(depth):
+    conv_one(nth(3), 1)
+    def close_block(origin):
         for part in range(2):
             total = q2[origin, part].astype(f32)
             for frm in range(1, chips):
                 total = total + q2[origin, 2 * frm + part].astype(f32)
-            at = pl.ds(origin * block + part * half, half)
+            at = pl.ds(pl.multiple_of(origin * block + part * half, half), half)
             value = total * act1[at, :]
             act1[at, :] = value
-            one.append(jnp.sum(value.reshape(2, GSIZE, lanes), axis=1))
-            two.append(jnp.sum((value * nrm1[at, :]).reshape(2, GSIZE, lanes), axis=1))
-    send_sums(1, pack_sums(jnp.concatenate(one, axis=0), jnp.concatenate(two, axis=0)))
+            sums_ref[0, origin, part] = jnp.sum(value.reshape(2, GSIZE, lanes), axis=1)
+            sums_ref[1, origin, part] = jnp.sum((value * nrm1[at, :]).reshape(2, GSIZE, lanes), axis=1)
+
+    span = q2.at[0 : depth - 1, 0 : rows - 1]
+    wait_group(span, span, o_send.at[0], o_recv.at[0])
+    for origin in (d, nth(1), nth(2)):
+        close_block(origin)
+    span = q2.at[0, 0 : rows - 1]
+    wait_group(span, span, o_send.at[0], o_recv.at[1])
+    close_block(nth(3))
+    one, two = [
+        jnp.concatenate([sums_ref[which, origin, part] for origin in range(depth) for part in range(2)], axis=0)
+        for which in range(2)
+    ]
+    send_sums(1, pack_sums(one, two))
     first1, second1 = wait_sums(1)
     value = spread(inverse1) * (act1[...] - spread(first1) - nrm1[...] * spread(second1))
     out_ref[...] = (cot_t[...].astype(f32) + value).astype(bf16).T
@@ -664,8 +672,7 @@
     sent(x_cot.at[0, 0 : chips - 1], c_send.at[0], c_recv.at[0])
     share(x_cot, 0).wait_send()
     sent(hid_two.at[0 : rows - 1], h_send.at[0], h_recv.at[0])
-    for which in range(2):
-        sent(st_b.at[which, 0 : rows - 1], t_send.at[which], t_recv.at[which])
+    sent(st_b.at[:, 0 : rows - 1], t_send.at[0], t_recv.at[0])
     sent(p2.at[:, 0 : rows - 1], o_send.at[0], o_recv.at[0])
     for count, here in ((chips - 1, own), (chips, jnp.logical_not(own))):
         @pl.when(here)
@@ -754,6 +761,7 @@
             pltpu.VMEM((2, groups // 2, lanes), f32),
             pltpu.VMEM((2, rows, groups // 2, lanes), f32),
             pltpu.VMEM((channels, 8), f32),
+            pltpu.VMEM((2, depth, 2, 2, lanes), f32),
             pltpu.VMEM((2, chips, block, lanes), bf16),
             pltpu.VMEM((rows, 2, GSIZE, lanes), bf16),
             pltpu.VMEM((rows, GSIZE, lanes), bf16),
@@ -764,14 +772,14 @@
             pltpu.VMEM((rows // 2, 2 * GSIZE, lanes), f32),
             pltpu.VMEM((rows // 2, 2 * GSIZE, lanes), bf16),
             pltpu.VMEM((2, rows // 2, 2 * GSIZE, lanes), bf16),
-            dma((2, 2, 2)), dma((2, depth, 2, 2)),
+            dma((2, 2, 2)), dma((2, depth - 1, 2, 2)),
             dma((1,)), dma((1,)),
             dma((2,)), dma((2,)),
             dma((2,)), dma((2,)),
             dma((2,)), dma((2,)),
             dma((2,)), dma((3,)),
-            dma((1,)), dma((depth,)),
-            dma((2,)), dma((2,)),
+            dma((1,)), dma((2,)),
+            dma((1,)), dma((2,)),
             dma((2,)), dma((2,)),
             dma((1,)), dma((1,)),
         ],

time: 42.2 us -> 42 us (level)
  no operation moved by 1% of the time
where the time goes in v6:
time: 42 us; the launch traced here: 41.9 us
  Pallas kernels  41.2 us (98%)
  local copies, waits for them, and re-layouts  0.67 us (2%)
    pallas_call x1, Pallas kernels, kernel_body(): pl.pallas_call(functools.partial(kernel, depth, rows, breadth), out_shape...  41.2 us

profile of v6, /device:TPU:0, one launch (start us, length us, event | category | flops | bytes accessed | tf_op | source)
XLA Modules:
  0.0 41.9 jit_solution(4798420871648660055)
XLA Ops:
  0.0 41.2 %shard_map.91 = bf16[128,640]{1,0:T(8,128)(2,1)S(1)} custom-call(bf16[128,640]{1,0:T(8,128)(2,1)} %bitcast.7, bf16[128,640]{1,0:T(8,128)(2,1)} %bitcast.8, bf16[128,640]{1,0:T(8,128)(2,1)} %bitcast.9, bf16[9,160,80]{2,1,0:T(8,128)(2,1)} %raw1_hbm.1, bf16[9,160,80]{2,1,0:T(8,128)(2,1)} %raw2_hbm.1, f32[640]{0:T(1024)} %gain1_hbm.1, f32[640]{0:T(1024)} %shift1_hbm.1, ...), custom_call_target="tpu_custom_call" | custom-call | tf_op jit(solution)/shard_map/pallas_call | solution.py:723
  41.2 0.7 %copy.12 = bf16[2,1,64,640]{3,2,1,0:T(8,128)(2,1)} copy(bf16[2,1,64,640]{3,2,1,0:T(8,128)(2,1)S(1)} %bitcast.6) | data formatting | bytes 327680

commit v7 on v6

--- a/solution.py
+++ b/solution.py
@@ -102,13 +102,13 @@
     depth, rows, breadth,
     lat_hbm, hid_hbm, cot_hbm, raw1_hbm, raw2_hbm, gain1_hbm, shift1_hbm, gain2_hbm, shift2_hbm,
     out_ref,
-    lat_ref, hid_ref, cot_ref, raw1, raw2, gain1, shift1, gain2, shift2, in_sem,
+    lat_ref, hid_ref, cot_ref, raw1, raw2, vectors, in_sem,
     cot_t, x_cot, hid_b, w1, w2, s1, s2, r1,
     xs1, xs2, y_ref, p1, q1, p2, q2, hg_s, hg_r,
     nrm1, act1, nrm2, act2, inv2_ref, st_s, st_b, par_ref,
     sums_ref, x_far, hid_two, hid_far, xs_far, p_far, q_far, nrm_far, act_far, hg_far, hg_two,
     z_send, z_recv, f_send, f_recv, b_send, b_recv, c_send, c_recv, h_send, h_recv,
-    p_send, p_recv, o_send, o_recv, t_send, t_recv, d_send, d_recv, e_send, e_recv,
+    p_send, p_recv, o_send, o_recv, t_send, t_recv, d_recv, e_send, e_recv,
 ):
     d = lax.axis_index("dp")
     r = lax.axis_index("rows")
@@ -136,10 +136,11 @@
         name: pltpu.make_async_copy(src, dst, in_sem.at[index])
         for index, (name, src, dst) in enumerate((
             ("raw2", raw2_hbm, raw2), ("cot", cot_hbm, cot_ref), ("hid", hid_hbm, hid_ref),
-            ("raw1", raw1_hbm, raw1), ("lat", lat_hbm, lat_ref), ("gain1", gain1_hbm, gain1),
-            ("shift1", shift1_hbm, shift1), ("gain2", gain2_hbm, gain2), ("shift2", shift2_hbm, shift2),
+            ("raw1", raw1_hbm, raw1), ("lat", lat_hbm, lat_ref),
         ))
     }
+    for index, src in enumerate((gain1_hbm, shift1_hbm, gain2_hbm, shift2_hbm)):
+        loads[index] = pltpu.make_async_copy(src, vectors.at[index, 0], in_sem.at[5])
     loads["raw2"].start()
 
     barrier = pltpu.get_barrier_semaphore()
@@ -190,8 +191,8 @@
         for at in range((tall - 128) // pad):
             ready[pad * at : pad * (at + 1), tall:] = ready[tall - pad :, 128 + pad * at : 128 + pad * (at + 1)]
 
-    def unpack(w, origin):
-        for part in range(2):
+    def unpack(w, origin, parts=(0, 1)):
+        for part in parts:
             pieces = [w[origin, part, pad * at : pad * (at + 1), tall:] for at in range((tall - 128) // pad)]
             full = jnp.concatenate(pieces + [jnp.zeros((pad, pad), bf16)], axis=1)
             w[origin, part, tall - pad :, 128:] = full
@@ -206,7 +207,7 @@
         deep, low, high = segments[seg]
         piece = w.at[origin, part, 0:deep, low:high]
         return remote(
-            piece, piece, z_send.at[which, way, seg], z_recv.at[which, origin - way, part, seg], dp=d + 1 - 2 * way
+            piece, piece, z_send.at[seg], z_recv.at[which, origin - way, part, seg], dp=d + 1 - 2 * way
         )
 
     near = jnp.minimum(d, depth - 1 - d)
@@ -236,26 +237,21 @@
                 copy.wait_recv()
                 copy.start()
 
-    def take(which, w, step, segs=(0, 1)):
-        for part in (k, 1 - k):
-            for seg in segs:
+    def take(which, w, step, parts=(k, 1 - k)):
+        for part in parts:
+            for seg in range(2):
                 origin = nth(step)
                 hop(which, w, origin, part, seg, jnp.where(origin > d, 1, 0)).wait_recv()
 
-    def take_end(which, w, step, segs=(0, 1)):
+    def take_end(which, w, step, parts=(k, 1 - k)):
         @pl.when(jnp.logical_not(middle))
         def _():
-            take(which, w, step, segs)
-
-    def wait_hops(which, w, spans):
-        for here, way, low, high in spans:
-            @pl.when(d == here)
-            def _():
-                for seg, (deep, left, right) in enumerate(segments):
-                    span = w.at[low:high, :, 0:deep, left:right]
-                    remote(
-                        span, span, z_send.at[which, way, seg], z_recv.at[which, 0, 0, 0], dp=d + 1 - 2 * way
-                    ).wait_send()
+            take(which, w, step, parts)
+
+    def wait_hops(count):
+        for seg, (deep, _, _) in enumerate(segments):
+            span = xs1.at[:, 0:count, 0:deep]
+            remote(span, span, z_send.at[seg], z_recv.at[0, 0, 0, seg], rows=sibling).wait_send()
 
     start_hops(0, w2, k, segs=(0,))
     pack(w2.at[d, k])
@@ -368,9 +364,8 @@
     nrm1[...] = lat_ref[...].astype(f32).T
     send_sums(0, pack_sums(by_group(nrm1[...]), by_group(nrm1[...] * nrm1[...])))
 
-    for name in ("gain1", "shift1", "gain2", "shift2"):
-        loads[name].wait()
-    raw_params = [p[...].reshape(1, channels) for p in (gain1, shift1, gain2, shift2)]
+    pltpu.make_async_copy(vectors, vectors, in_sem.at[5]).wait()
+    raw_params = [vectors[index] for index in range(4)]
     par_ref[...] = jnp.concatenate(raw_params + raw_params, axis=0).T
 
     def store_shifts(xs, part, h, values):
@@ -388,7 +383,7 @@
     wait_group(everyone, everyone, c_send.at[0], c_recv.at[0])
 
     def share(x, at):
-        return remote(x.at[k], x.at[k], d_send.at[at], d_recv.at[at], rows=sibling)
+        return remote(x.at[k], x.at[k], c_send.at[1], d_recv.at[at], rows=sibling)
 
     def shift_rows(x, xs):
         for h in range(rows):
@@ -451,8 +446,19 @@
     def conv_far(step):
         conv_two(nth(step), xs_far, p_far.at[step - 2], q_far, p_send.at[1], p_recv.at[2])
 
+    def conv_half(origin, part, more):
+        for h in range(0, rows, 2):
+            pair = jnp.concatenate([xs1[part, h], xs1[part, h + 1]], axis=1)
+            term = jnp.dot(w1[origin, part], pair, preferred_element_type=f32)
+            for side in range(2):
+                value = term[:, side * lanes : (side + 1) * lanes]
+                y_ref[h + side] = y_ref[h + side] + value if more else value
+
     def conv_one(origin, last=0):
         conv(w1, origin, xs1)
+        send_rows(origin, last)
+
+    def send_rows(origin, last=0):
         for h in range(rows):
             p2[origin, h] = row_of(h).astype(bf16)
         for off in range(1, rows):
@@ -620,12 +626,14 @@
     for h in range(rows):
         store_shifts(xs1, k, h, hg_s[h].astype(f32))
     forward(1, w1, 3, 0)
+    conv_half(d, k, False)
     swap.wait_recv()
     for h in range(rows):
         store_shifts(xs1, 1 - k, h, hg_r[h].astype(f32))
 
     forward(1, w1, 3, 1)
-    conv_one(d)
+    conv_half(d, 1 - k, True)
+    send_rows(d)
     forward(1, w1, 3, 2)
     take_end(1, w1, 1)
     unpack(w1, nth(1))
@@ -634,9 +642,13 @@
     take_end(1, w1, 2)
     unpack(w1, nth(2))
     conv_one(nth(2))
-    take_end(1, w1, 3)
-    unpack(w1, nth(3))
-    conv_one(nth(3), 1)
+    take_end(1, w1, 3, (k,))
+    unpack(w1, nth(3), (k,))
+    conv_half(nth(3), k, False)
+    take_end(1, w1, 3, (1 - k,))
+    unpack(w1, nth(3), (1 - k,))
+    conv_half(nth(3), 1 - k, True)
+    send_rows(nth(3), 1)
     def close_block(origin):
         for part in range(2):
             total = q2[origin, part].astype(f32)
@@ -670,7 +682,7 @@
         remote(span, span, send, recv, rows=sibling).wait_send()
 
     sent(x_cot.at[0, 0 : chips - 1], c_send.at[0], c_recv.at[0])
-    share(x_cot, 0).wait_send()
+    sent(x_far, c_send.at[1], d_recv.at[0])
     sent(hid_two.at[0 : rows - 1], h_send.at[0], h_recv.at[0])
     sent(st_b.at[:, 0 : rows - 1], t_send.at[0], t_recv.at[0])
     sent(p2.at[:, 0 : rows - 1], o_send.at[0], o_recv.at[0])
@@ -690,20 +702,19 @@
 
     @pl.when(middle)
     def _():
-        share(x_far, 1).wait_send()
         lend.wait_send()
 
     @pl.when(jnp.logical_not(middle))
     def _():
-        lend_cot.wait_send()
         lend_hid.wait_send()
 
-    last = depth - 1
-    wait_hops(0, w2, [(0, 0, 0, 1), (1, 0, 0, 2), (1, 1, 1, 2), (2, 0, 2, 3), (2, 1, 2, 4), (3, 1, 3, 4)])
-    wait_hops(
-        1, w1,
-        [(here, 0, 0, here + 1) for here in range(last)] + [(here, 1, here, depth) for here in range(1, depth)],
-    )
+    @pl.when(middle)
+    def _():
+        wait_hops(2 * depth)
+
+    @pl.when(jnp.logical_not(middle))
+    def _():
+        wait_hops(2)
 
 
 def kernel_body(
@@ -731,11 +742,8 @@
             pltpu.VMEM((lanes, channels), bf16),
             pltpu.VMEM(filter_one.shape, bf16),
             pltpu.VMEM(filter_two.shape, bf16),
-            pltpu.VMEM((channels,), f32),
-            pltpu.VMEM((channels,), f32),
-            pltpu.VMEM((channels,), f32),
-            pltpu.VMEM((channels,), f32),
-            dma((9,)),
+            pltpu.VMEM((4, 1, channels), f32),
+            dma((6,)),
             pltpu.VMEM((channels, lanes), bf16),
             pltpu.VMEM((2, chips, block, lanes), bf16),
             pltpu.VMEM((2, rows, GSIZE, lanes), bf16),
@@ -772,7 +780,7 @@
             pltpu.VMEM((rows // 2, 2 * GSIZE, lanes), f32),
             pltpu.VMEM((rows // 2, 2 * GSIZE, lanes), bf16),
             pltpu.VMEM((2, rows // 2, 2 * GSIZE, lanes), bf16),
-            dma((2, 2, 2)), dma((2, depth - 1, 2, 2)),
+            dma((2,)), dma((2, depth - 1, 2, 2)),
             dma((1,)), dma((1,)),
             dma((2,)), dma((2,)),
             dma((2,)), dma((2,)),
@@ -780,7 +788,7 @@
             dma((2,)), dma((3,)),
             dma((1,)), dma((2,)),
             dma((1,)), dma((2,)),
-            dma((2,)), dma((2,)),
+            dma((2,)),
             dma((1,)), dma((1,)),
         ],
         compiler_params=pltpu.CompilerParams(

time: 42 us -> 41.8 us (level)
  no operation moved by 1% of the time
where the time goes in v7:
time: 41.8 us; the launch traced here: 41.6 us
  Pallas kernels  41 us (98%)
  local copies, waits for them, and re-layouts  0.67 us (2%)
    pallas_call x1, Pallas kernels, kernel_body(): pl.pallas_call(functools.partial(kernel, depth, rows, breadth), out_shape...  41 us

profile of v7, /device:TPU:0, one launch (start us, length us, event | category | flops | bytes accessed | tf_op | source)
XLA Modules:
  0.0 41.6 jit_solution(10532819264450610643)
XLA Ops:
  0.0 41.0 %shard_map.91 = bf16[128,640]{1,0:T(8,128)(2,1)S(1)} custom-call(bf16[128,640]{1,0:T(8,128)(2,1)} %bitcast.7, bf16[128,640]{1,0:T(8,128)(2,1)} %bitcast.8, bf16[128,640]{1,0:T(8,128)(2,1)} %bitcast.9, bf16[9,160,80]{2,1,0:T(8,128)(2,1)} %raw1_hbm.1, bf16[9,160,80]{2,1,0:T(8,128)(2,1)} %raw2_hbm.1, f32[640]{0:T(1024)} %gain1_hbm.1, f32[640]{0:T(1024)} %shift1_hbm.1, ...), custom_call_target="tpu_custom_call" | custom-call | tf_op jit(solution)/shard_map/pallas_call | solution.py:734
  41.0 0.7 %copy.12 = bf16[2,1,64,640]{3,2,1,0:T(8,128)(2,1)} copy(bf16[2,1,64,640]{3,2,1,0:T(8,128)(2,1)S(1)} %bitcast.6) | data formatting | bytes 327680

commit v8 on v7

--- a/solution.py
+++ b/solution.py
@@ -627,18 +627,18 @@
         store_shifts(xs1, k, h, hg_s[h].astype(f32))
     forward(1, w1, 3, 0)
     conv_half(d, k, False)
+    forward(1, w1, 3, 1)
+    forward(1, w1, 3, 2)
+    forward(1, w1, 3, 3)
     swap.wait_recv()
     for h in range(rows):
         store_shifts(xs1, 1 - k, h, hg_r[h].astype(f32))
 
-    forward(1, w1, 3, 1)
     conv_half(d, 1 - k, True)
     send_rows(d)
-    forward(1, w1, 3, 2)
     take_end(1, w1, 1)
     unpack(w1, nth(1))
     conv_one(nth(1))
-    forward(1, w1, 3, 3)
     take_end(1, w1, 2)
     unpack(w1, nth(2))
     conv_one(nth(2))

time: 41.8 us -> 41.8 us (level)
  no operation moved by 1% of the time
where the time goes in v8:
time: 41.8 us; the launch traced here: 41.6 us
  Pallas kernels  41 us (98%)
  local copies, waits for them, and re-layouts  0.67 us (2%)
    pallas_call x1, Pallas kernels, kernel_body(): pl.pallas_call(functools.partial(kernel, depth, rows, breadth), out_shape...  41 us

profile of v8, /device:TPU:0, one launch (start us, length us, event | category | flops | bytes accessed | tf_op | source)
XLA Modules:
  0.0 41.6 jit_solution(3336835133657183912)
XLA Ops:
  0.0 41.0 %shard_map.91 = bf16[128,640]{1,0:T(8,128)(2,1)S(1)} custom-call(bf16[128,640]{1,0:T(8,128)(2,1)} %bitcast.7, bf16[128,640]{1,0:T(8,128)(2,1)} %bitcast.8, bf16[128,640]{1,0:T(8,128)(2,1)} %bitcast.9, bf16[9,160,80]{2,1,0:T(8,128)(2,1)} %raw1_hbm.1, bf16[9,160,80]{2,1,0:T(8,128)(2,1)} %raw2_hbm.1, f32[640]{0:T(1024)} %gain1_hbm.1, f32[640]{0:T(1024)} %shift1_hbm.1, ...), custom_call_target="tpu_custom_call" | custom-call | tf_op jit(solution)/shard_map/pallas_call | solution.py:734
  41.0 0.7 %copy.12 = bf16[2,1,64,640]{3,2,1,0:T(8,128)(2,1)} copy(bf16[2,1,64,640]{3,2,1,0:T(8,128)(2,1)S(1)} %bitcast.6) | data formatting | bytes 327680

commit v9 on v8

--- a/solution.py
+++ b/solution.py
@@ -124,6 +124,8 @@
     number = rows * breadth * GSIZE
     groups = channels // GSIZE
     bf16, f32 = jnp.bfloat16, jnp.float32
+    across, along, beside = chips - 1 - c, lax.rem(c + 2, chips), c + 1 - 2 * lax.rem(c, 2)
+    others = [2 * across + k, 2 * beside + k, 2 * across + 1 - k, 2 * beside + 1 - k, 2 * along + k, 2 * along + 1 - k, sibling]
 
     def remote(src, dst, send, recv, **device):
         return pltpu.make_async_remote_copy(
@@ -336,8 +338,7 @@
 
     def send_sums(which, packed):
         st_s[which] = packed
-        for off in range(1, rows):
-            to = lax.rem(r + off, rows)
+        for to in others:
             remote(st_s.at[which], st_b.at[which, r], t_send.at[0], t_recv.at[which], rows=to).start()
         st_b[which, r] = packed
 
@@ -461,8 +462,7 @@
     def send_rows(origin, last=0):
         for h in range(rows):
             p2[origin, h] = row_of(h).astype(bf16)
-        for off in range(1, rows):
-            to = lax.rem(r + off, rows)
+        for to in others:
             remote(p2.at[origin, to], q2.at[origin, r], o_send.at[0], o_recv.at[last], rows=to).start()
         q2[origin, r] = p2[origin, r]
 

time: 41.8 us -> 41.8 us (level)
  no operation moved by 1% of the time
where the time goes in v9:
time: 41.8 us; the launch traced here: 41.6 us
  Pallas kernels  41 us (98%)
  local copies, waits for them, and re-layouts  0.67 us (2%)
    pallas_call x1, Pallas kernels, kernel_body(): pl.pallas_call(functools.partial(kernel, depth, rows, breadth), out_shape...  41 us

profile of v9, /device:TPU:0, one launch (start us, length us, event | category | flops | bytes accessed | tf_op | source)
XLA Modules:
  0.0 41.6 jit_solution(232807332839711833)
XLA Ops:
  0.0 41.0 %shard_map.91 = bf16[128,640]{1,0:T(8,128)(2,1)S(1)} custom-call(bf16[128,640]{1,0:T(8,128)(2,1)} %bitcast.7, bf16[128,640]{1,0:T(8,128)(2,1)} %bitcast.8, bf16[128,640]{1,0:T(8,128)(2,1)} %bitcast.9, bf16[9,160,80]{2,1,0:T(8,128)(2,1)} %raw1_hbm.1, bf16[9,160,80]{2,1,0:T(8,128)(2,1)} %raw2_hbm.1, f32[640]{0:T(1024)} %gain1_hbm.1, f32[640]{0:T(1024)} %shift1_hbm.1, ...), custom_call_target="tpu_custom_call" | custom-call | tf_op jit(solution)/shard_map/pallas_call | solution.py:734
  41.0 0.7 %copy.12 = bf16[2,1,64,640]{3,2,1,0:T(8,128)(2,1)} copy(bf16[2,1,64,640]{3,2,1,0:T(8,128)(2,1)S(1)} %bitcast.6) | data formatting | bytes 327680
